TPU v7x, 128 devices: a whole 4x4x4 slice. The times are simulated.
128 devices in a mesh: dp: 1, cp: 128 (over z, y, x, core).
Axes of the slice: x: 4, y: 4, z: 4, core: 2. Of those that a mesh axis runs over, the one named last changes fastest.
Arguments:
- hidden: bfloat16 [65536, 3072], P(('dp', 'cp'))
- w_q: bfloat16 [3072, 24, 128], replicated
- w_k: bfloat16 [3072, 2, 128], replicated
- w_v: bfloat16 [3072, 2, 128], replicated
- w_o: bfloat16 [24, 128, 3072], replicated
Outputs:
- output: bfloat16 [65536, 3072], P(('dp', 'cp'))
All inputs are finite; a program needn't handle non-finite values.
Results may differ from a plain program's by a relative error of at most 0.00541686.
Values are sent between devices in bfloat16 or wider.
A program may use at most 1 GiB of HBM per device.

v0:
```python
import jax
import jax.numpy as jnp
from jax import lax
from jax.sharding import PartitionSpec as P

WINDOW = 4096
ROPE_BASE = 10000.0


def rotate(values, positions, factor):
    half_dim = values.shape[-1] // 2
    inv_freq = 1.0 / (ROPE_BASE ** (jnp.arange(half_dim, dtype=jnp.float32) * (2.0 / values.shape[-1])))
    angles = positions.astype(jnp.float32)[..., None, None] * inv_freq
    cos_part = jnp.cos(angles)
    sin_part = jnp.sin(angles)
    first_half = values[..., :half_dim].astype(jnp.float32)
    second_half = values[..., half_dim:].astype(jnp.float32)
    rotated = jnp.concatenate([first_half * cos_part - second_half * sin_part, second_half * cos_part + first_half * sin_part], axis=-1)
    return (rotated * factor).astype(jnp.bfloat16)


def band_attention(queries, key_band, val_band, first_pos):
    chunk_len = queries.shape[1]
    band_len = key_band.shape[1] - chunk_len
    q_block = min(chunk_len, 128)
    key_span = band_len + q_block
    row_ids = jnp.arange(q_block)[:, None]
    col_ids = jnp.arange(key_span)[None, :]
    in_band = (col_ids > row_ids) & (col_ids <= row_ids + band_len)

    def one_block(block_id):
        row_start = block_id * q_block
        q_part = lax.dynamic_slice_in_dim(queries, row_start, q_block, axis=1)
        k_part = lax.dynamic_slice_in_dim(key_band, row_start, key_span, axis=1)
        v_part = lax.dynamic_slice_in_dim(val_band, row_start, key_span, axis=1)
        key_pos = first_pos[:, None] + row_start + jnp.arange(key_span)[None, :]
        allowed = in_band[None, :, :] & (key_pos >= 0)[:, None, :]
        scores = jnp.einsum('nqkgd,nskd->nkgqs', q_part, k_part, preferred_element_type=jnp.float32)
        scores = jnp.where(allowed[:, None, None, :, :], scores, -jnp.inf)
        row_max = jnp.max(scores, axis=-1, keepdims=True)
        exp_scores = jnp.exp(scores - row_max)
        row_sum = jnp.sum(exp_scores, axis=-1)
        attn_out = jnp.einsum('nkgqs,nskd->nqkgd', exp_scores.astype(jnp.bfloat16), v_part, preferred_element_type=jnp.float32)
        attn_out = attn_out / jnp.transpose(row_sum, (0, 3, 1, 2))[..., None]
        return attn_out.astype(jnp.bfloat16)

    blocks = lax.map(one_block, jnp.arange(chunk_len // q_block))
    return jnp.moveaxis(blocks, 0, 1).reshape(queries.shape)


def solution(mesh):
    cp_size = mesh.shape['cp']

    def device_step(hidden, w_q, w_k, w_v, w_o):
        my_index = lax.axis_index('cp')
        chunk_len = hidden.shape[0] // 2
        model_dim = hidden.shape[1]
        heads, head_dim = w_q.shape[1], w_q.shape[2]
        kv_heads = w_k.shape[1]
        group_size = heads // kv_heads
        win_chunks = WINDOW // chunk_len
        x_halves = hidden.reshape(2, chunk_len, model_dim)
        chunk_ids = jnp.stack([my_index, 2 * cp_size - 1 - my_index])
        positions = chunk_ids[:, None] * chunk_len + jnp.arange(chunk_len)[None, :]
        key_proj = jnp.einsum('nqd,dhe->nqhe', x_halves, w_k, preferred_element_type=jnp.float32).astype(jnp.bfloat16)
        val_proj = jnp.einsum('nqd,dhe->nqhe', x_halves, w_v, preferred_element_type=jnp.float32).astype(jnp.bfloat16)
        kv_pairs = jnp.stack([rotate(key_proj, positions, 1.0), val_proj], axis=1)
        kv_first = kv_pairs[0]
        kv_second = kv_pairs[1]
        from_below = []
        from_above = []
        from_fold = []
        for offset in range(1, win_chunks + 1):
            from_below.append(lax.ppermute(kv_first, 'cp', [(sender, sender + offset) for sender in range(cp_size - offset)]))
            from_above.append(lax.ppermute(kv_second, 'cp', [(sender, sender - offset) for sender in range(offset, cp_size)]))
            fold_pairs = [(sender, 2 * cp_size - 1 - sender - offset) for sender in range(cp_size - offset, cp_size) if 2 * cp_size - 1 - sender - offset != sender]
            if fold_pairs:
                from_fold.append(lax.ppermute(kv_first, 'cp', fold_pairs))
            else:
                from_fold.append(jnp.zeros_like(kv_first))
        upper_slots = []
        for offset in range(1, win_chunks + 1):
            fold_or_self = jnp.where(2 * cp_size - 1 - my_index - offset == my_index, kv_first, from_fold[offset - 1])
            upper_slots.append(jnp.where(my_index + offset < cp_size, from_above[offset - 1], fold_or_self))
        band_low = jnp.concatenate(from_below[::-1] + [kv_first], axis=1)
        band_high = jnp.concatenate(upper_slots[::-1] + [kv_second], axis=1)
        bands = jnp.stack([band_low, band_high], axis=1)
        q_proj = jnp.einsum('nqd,dhe->nqhe', x_halves, w_q, preferred_element_type=jnp.float32).astype(jnp.bfloat16)
        queries = rotate(q_proj, positions, head_dim ** -0.5).reshape(2, chunk_len, kv_heads, group_size, head_dim)
        first_pos = (chunk_ids - win_chunks) * chunk_len
        attended = band_attention(queries, bands[0], bands[1], first_pos)
        w_out = w_o.reshape(kv_heads, group_size, head_dim, model_dim)
        out_rows = jnp.einsum('nqkge,kgem->nqm', attended, w_out, preferred_element_type=jnp.float32)
        return out_rows.astype(jnp.bfloat16).reshape(2 * chunk_len, model_dim)

    return jax.shard_map(device_step, mesh=mesh, in_specs=(P(('dp', 'cp'), None), P(), P(), P(), P()), out_specs=P(('dp', 'cp'), None), check_vma=False)
```

profile of v0, /device:TPU:1, one launch (start us, length us, event | category | flops | bytes accessed | tf_op | source)
XLA Modules:
  0.0 598.7 jit_solution(12730328754454165815)
XLA Ops:
  22.8 24.3 %copy.21 = bf16[3072,24,128]{0,2,1:T(8,128)(2,1)} copy(bf16[3072,24,128]{2,1,0:T(8,128)(2,1)} %param.8) | data formatting | bytes 37748736 | tf_op args[1]
  47.1 13.9 %fusion.36 = bf16[2,256,24,128]{1,3,2,0:T(8,128)(2,1)S(1)} fusion(bf16[2,256,3072,1]{2,1,3,0:T(8,128)(2,1)S(1)} %bitcast.161, bf16[3072,24,128]{0,2,1:T(8,128)(2,1)} %copy.21), kind=kOutput, calls=%fused_computation.44 | convolution fusion | flops 9665249280 | bytes 25165824 | tf_op jit(solution)/shard_map/nqd,dhe->nqhe/dot_general | solution.py:88
  88.0 10.5 %collective-permute-done.20 = bf16[2,256,2,128]{1,3,2,0:T(8,128)(2,1)S(1)} collective-permute-done((bf16[2,256,2,128]{1,3,2,0:T(8,128)(2,1)}, bf16[2,256,2,128]{1,3,2,0:T(8,128)(2,1)S(1)}, u32[]{:S(2)}, u32[]{:S(2)}) %collective-permute-start.20) | collective-permute-done | bytes 262176 | tf_op jit(solution)/shard_map/ppermute | solution.py:75
  103.3 8.3 %collective-permute-done.24 = bf16[2,256,2,128]{1,3,2,0:T(8,128)(2,1)S(1)} collective-permute-done((bf16[2,256,2,128]{1,3,2,0:T(8,128)(2,1)}, bf16[2,256,2,128]{1,3,2,0:T(8,128)(2,1)S(1)}, u32[]{:S(2)}, u32[]{:S(2)}) %collective-permute-start.24) | collective-permute-done | bytes 262176 | tf_op jit(solution)/shard_map/ppermute | solution.py:75
  134.1 41.5 %collective-permute-start.36 = (bf16[2,256,2,128]{1,3,2,0:T(8,128)(2,1)}, bf16[2,256,2,128]{1,3,2,0:T(8,128)(2,1)S(1)}, u32[]{:S(2)}, u32[]{:S(2)}) collective-permute-start(bf16[2,256,2,128]{1,3,2,0:T(8,128)(2,1)} %get-tuple-element.107), channel_id=1, source_target_pairs={{6,0},{7,1},{8,2},{9,3},{10,4},{11,5},{12,6},{13,7},{14,8},{15,9},... | collective-permute-start | bytes 786440 | tf_op jit(solution)/shard_map/ppermute | solution.py:75
  176.5 12.1 %collective-permute-start.38 = (bf16[2,256,2,128]{1,3,2,0:T(8,128)(2,1)}, bf16[2,256,2,128]{1,3,2,0:T(8,128)(2,1)S(1)}, u32[]{:S(2)}, u32[]{:S(2)}) collective-permute-start(bf16[2,256,2,128]{1,3,2,0:T(8,128)(2,1)} %get-tuple-element.107), channel_id=1, source_target_pairs={{5,0},{6,1},{7,2},{8,3},{9,4},{10,5},{11,6},{12,7},{13,8},{14,9},{... | collective-permute-start | bytes 786440 | tf_op jit(solution)/shard_map/ppermute | solution.py:75
  189.3 12.4 %collective-permute-start.40 = (bf16[2,256,2,128]{1,3,2,0:T(8,128)(2,1)}, bf16[2,256,2,128]{1,3,2,0:T(8,128)(2,1)S(1)}, u32[]{:S(2)}, u32[]{:S(2)}) collective-permute-start(bf16[2,256,2,128]{1,3,2,0:T(8,128)(2,1)} %get-tuple-element.107), channel_id=1, source_target_pairs={{4,0},{5,1},{6,2},{7,3},{8,4},{9,5},{10,6},{11,7},{12,8},{13,9},{1... | collective-permute-start | bytes 786440 | tf_op jit(solution)/shard_map/ppermute | solution.py:75
  202.5 12.1 %collective-permute-start.42 = (bf16[2,256,2,128]{1,3,2,0:T(8,128)(2,1)}, bf16[2,256,2,128]{1,3,2,0:T(8,128)(2,1)S(1)}, u32[]{:S(2)}, u32[]{:S(2)}) collective-permute-start(bf16[2,256,2,128]{1,3,2,0:T(8,128)(2,1)} %get-tuple-element.107), channel_id=1, source_target_pairs={{3,0},{4,1},{5,2},{6,3},{7,4},{8,5},{9,6},{10,7},{11,8},{12,9},{13... | collective-permute-start | bytes 786440 | tf_op jit(solution)/shard_map/ppermute | solution.py:75
  247.7 16.8 %collective-permute-start.7 = (bf16[2,256,2,128]{1,3,2,0:T(8,128)(2,1)}, bf16[2,256,2,128]{1,3,2,0:T(8,128)(2,1)S(1)}, u32[]{:S(2)}, u32[]{:S(2)}) collective-permute-start(bf16[2,256,2,128]{1,3,2,0:T(8,128)(2,1)} %get-tuple-element.108), channel_id=1, source_target_pairs={{0,9},{1,10},{2,11},{3,12},{4,13},{5,14},{6,15},{7,16},{8,17},{9,1... | collective-permute-start | bytes 786440 | tf_op jit(solution)/shard_map/ppermute | solution.py:74
  269.0 17.2 %collective-permute-start.11 = (bf16[2,256,2,128]{1,3,2,0:T(8,128)(2,1)}, bf16[2,256,2,128]{1,3,2,0:T(8,128)(2,1)S(1)}, u32[]{:S(2)}, u32[]{:S(2)}) collective-permute-start(bf16[2,256,2,128]{1,3,2,0:T(8,128)(2,1)} %get-tuple-element.108), channel_id=1, source_target_pairs={{0,5},{1,6},{2,7},{3,8},{4,9},{5,10},{6,11},{7,12},{8,13},{9,14},{... | collective-permute-start | bytes 786440 | tf_op jit(solution)/shard_map/ppermute | solution.py:74
  286.3 10.2 %collective-permute-start.12 = (bf16[2,256,2,128]{1,3,2,0:T(8,128)(2,1)}, bf16[2,256,2,128]{1,3,2,0:T(8,128)(2,1)S(1)}, u32[]{:S(2)}, u32[]{:S(2)}) collective-permute-start(bf16[2,256,2,128]{1,3,2,0:T(8,128)(2,1)} %get-tuple-element.108), channel_id=1, source_target_pairs={{0,4},{1,5},{2,6},{3,7},{4,8},{5,9},{6,10},{7,11},{8,12},{9,13},{1... | collective-permute-start | bytes 786440 | tf_op jit(solution)/shard_map/ppermute | solution.py:74
  296.5 10.2 %collective-permute-start.13 = (bf16[2,256,2,128]{1,3,2,0:T(8,128)(2,1)}, bf16[2,256,2,128]{1,3,2,0:T(8,128)(2,1)S(1)}, u32[]{:S(2)}, u32[]{:S(2)}) collective-permute-start(bf16[2,256,2,128]{1,3,2,0:T(8,128)(2,1)} %get-tuple-element.108), channel_id=1, source_target_pairs={{0,3},{1,4},{2,5},{3,6},{4,7},{5,8},{6,9},{7,10},{8,11},{9,12},{10... | collective-permute-start | bytes 786440 | tf_op jit(solution)/shard_map/ppermute | solution.py:74
  306.7 10.2 %collective-permute-start.14 = (bf16[2,256,2,128]{1,3,2,0:T(8,128)(2,1)}, bf16[2,256,2,128]{1,3,2,0:T(8,128)(2,1)S(1)}, u32[]{:S(2)}, u32[]{:S(2)}) collective-permute-start(bf16[2,256,2,128]{1,3,2,0:T(8,128)(2,1)} %get-tuple-element.108), channel_id=1, source_target_pairs={{0,2},{1,3},{2,4},{3,5},{4,6},{5,7},{6,8},{7,9},{8,10},{9,11},{10,... | collective-permute-start | bytes 786440 | tf_op jit(solution)/shard_map/ppermute | solution.py:74
  317.0 10.2 %collective-permute-start.15 = (bf16[2,256,2,128]{1,3,2,0:T(8,128)(2,1)}, bf16[2,256,2,128]{1,3,2,0:T(8,128)(2,1)S(1)}, u32[]{:S(2)}, u32[]{:S(2)}) collective-permute-start(bf16[2,256,2,128]{1,3,2,0:T(8,128)(2,1)} %get-tuple-element.108), channel_id=1, source_target_pairs={{0,1},{1,2},{2,3},{3,4},{4,5},{5,6},{6,7},{7,8},{8,9},{9,10},{10,1... | collective-permute-start | bytes 786440 | tf_op jit(solution)/shard_map/ppermute | solution.py:74
  327.2 9.5 %collective-permute-start.44 = (bf16[2,256,2,128]{1,3,2,0:T(8,128)(2,1)}, bf16[2,256,2,128]{1,3,2,0:T(8,128)(2,1)S(1)}, u32[]{:S(2)}, u32[]{:S(2)}) collective-permute-start(bf16[2,256,2,128]{1,3,2,0:T(8,128)(2,1)} %get-tuple-element.107), channel_id=1, source_target_pairs={{2,0},{3,1},{4,2},{5,3},{6,4},{7,5},{8,6},{9,7},{10,8},{11,9},{12,... | collective-permute-start | bytes 786440 | tf_op jit(solution)/shard_map/ppermute | solution.py:75
  337.5 11.7 %collective-permute-start.46 = (bf16[2,256,2,128]{1,3,2,0:T(8,128)(2,1)}, bf16[2,256,2,128]{1,3,2,0:T(8,128)(2,1)S(1)}, u32[]{:S(2)}, u32[]{:S(2)}) collective-permute-start(bf16[2,256,2,128]{1,3,2,0:T(8,128)(2,1)} %get-tuple-element.107), channel_id=1, source_target_pairs={{1,0},{2,1},{3,2},{4,3},{5,4},{6,5},{7,6},{8,7},{9,8},{10,9},{11,1... | collective-permute-start | bytes 786440 | tf_op jit(solution)/shard_map/ppermute | solution.py:75
  358.8 225.1 %while.11 = (s32[]{:T(128)}, bf16[2,2,128,2,12,128]{5,2,0,4,1,3:T(8,128)(2,1)}, s32[2]{0:T(128)S(1)}, bf16[2,4352,2,128]{1,3,2,0:T(8,128)(2,1)}, s32[2]{0:T(128)...) while((s32[]{:T(128)}, ...), condition=%wide.region_3.4_spmd.clone, body=%wide.region_0.3_spmd.clone.sunk | while | flops 13499453440 | bytes 335062752 | solution.py:47
  362.3 38.4 %fusion.73 = (f32[2,2,12,128]{3,2,1,0:T(8,128)S(1)}, f32[2,2,4224,128,12]{3,2,4,1,0:T(8,128)}) fusion(pred[2,128,4224]{1,2,0:T(8,128)(4,1)S(1)} %broadcast_and_fusion.2, bf16[2,256,2,12,128]{4,1,3,2,0:T(8,128)(2,1)} %get-tuple-element.200, s32[]{:T(128)S(6)} %select_n.358, bf16[2,4352,2,128]{1,3,2,0:T(8,128)(2,1)} %get-tuple-element.199, ...), kind=kOutput, calls=%fused_computation.3.clone.1 | convolution fusion | flops 6695675904 | bytes 110813192 | tf_op jit(solution)/shard_map/while/body/eval_jaxpr/nqkgd,nskd->nkgqs/dot_general | solution.py:38
  400.6 32.0 %fusion.74 = f32[2,2,12,128]{3,2,1,0:T(8,128)S(1)} fusion(f32[2,2,4224,128,12]{3,2,4,1,0:T(8,128)} %get-tuple-element.166, f32[2,2,12,128]{3,2,1,0:T(8,128)S(1)} %get-tuple-element.167, pred[2,128,4224]{1,2,0:T(8,128)(4,1)S(1)} %broadcast_and_fusion.2), kind=kLoop, calls=%fused_computation.4.clone.1 | loop fusion | flops 77850624 | bytes 104939520 | tf_op jit(solution)/shard_map/while/body/eval_jaxpr/reduce_sum | solution.py:42
  432.7 36.1 %fusion.75 = bf16[1,2,128,2,12,128]{2,5,4,3,1,0:T(8,128)(2,1)S(1)} fusion(f32[2,128,2,12]{1,3,2,0:T(8,128)S(1)} %bitcast.166, f32[2,2,4224,128,12]{3,2,4,1,0:T(8,128)} %get-tuple-element.166, f32[2,2,12,128]{3,2,1,0:T(8,128)S(1)} %get-tuple-element.167, pred[2,128,4224]{1,2,0:T(8,128)(4,1)S(1)} %broadcast_and_fusion.2, ...), kind=kOutput, calls=%fused_computation.20.clone.1 | convolution fusion | flops 6723207168 | bytes 110837760 | tf_op jit(solution)/shard_map/while/body/eval_jaxpr/nkgqs,nskd->nqkgd/dot_general | solution.py:43
  474.8 38.4 %fusion.73 = (f32[2,2,12,128]{3,2,1,0:T(8,128)S(1)}, f32[2,2,4224,128,12]{3,2,4,1,0:T(8,128)}) fusion(pred[2,128,4224]{1,2,0:T(8,128)(4,1)S(1)} %broadcast_and_fusion.2, bf16[2,256,2,12,128]{4,1,3,2,0:T(8,128)(2,1)} %get-tuple-element.200, s32[]{:T(128)S(6)} %select_n.358, bf16[2,4352,2,128]{1,3,2,0:T(8,128)(2,1)} %get-tuple-element.199, ...), kind=kOutput, calls=%fused_computation.3.clone.1 | convolution fusion | flops 6695675904 | bytes 110813192 | tf_op jit(solution)/shard_map/while/body/eval_jaxpr/nqkgd,nskd->nkgqs/dot_general | solution.py:38
  513.2 32.0 %fusion.74 = f32[2,2,12,128]{3,2,1,0:T(8,128)S(1)} fusion(f32[2,2,4224,128,12]{3,2,4,1,0:T(8,128)} %get-tuple-element.166, f32[2,2,12,128]{3,2,1,0:T(8,128)S(1)} %get-tuple-element.167, pred[2,128,4224]{1,2,0:T(8,128)(4,1)S(1)} %broadcast_and_fusion.2), kind=kLoop, calls=%fused_computation.4.clone.1 | loop fusion | flops 77850624 | bytes 104939520 | tf_op jit(solution)/shard_map/while/body/eval_jaxpr/reduce_sum | solution.py:42
  545.2 36.1 %fusion.75 = bf16[1,2,128,2,12,128]{2,5,4,3,1,0:T(8,128)(2,1)S(1)} fusion(f32[2,128,2,12]{1,3,2,0:T(8,128)S(1)} %bitcast.166, f32[2,2,4224,128,12]{3,2,4,1,0:T(8,128)} %get-tuple-element.166, f32[2,2,12,128]{3,2,1,0:T(8,128)S(1)} %get-tuple-element.167, pred[2,128,4224]{1,2,0:T(8,128)(4,1)S(1)} %broadcast_and_fusion.2, ...), kind=kOutput, calls=%fused_computation.20.clone.1 | convolution fusion | flops 6723207168 | bytes 110837760 | tf_op jit(solution)/shard_map/while/body/eval_jaxpr/nkgqs,nskd->nqkgd/dot_general | solution.py:43
  583.9 14.8 %bitcast_convert_fusion = bf16[2,256,3072]{2,1,0:T(8,128)(2,1)} fusion(bf16[2,256,2,12,128]{4,1,3,0,2:T(8,128)(2,1)} %bitcast.168, bf16[2,12,128,3072,1]{3,2,1,4,0:T(8,128)(2,1)} %bitcast.167), kind=kOutput, calls=%fused_computation.33 | convolution fusion | flops 9665249280 | bytes 25165824 | tf_op jit(solution)/shard_map/nqkge,kgem->nqm/dot_general | solution.py:93
  (155 shorter events, 137.6 us)
Async XLA Ops:
  11.1 224.7 %collective-permute-start = (bf16[2,256,2,128]{1,3,2,0:T(8,128)(2,1)}, bf16[2,256,2,128]{1,3,2,0:T(8,128)(2,1)}, u32[]{:S(2)}, u32[]{:S(2)}) collective-permute-start(bf16[2,256,2,128]{1,3,2,0:T(8,128)(2,1)} %get-tuple-element.108), channel_id=1, source_target_pairs={{0,16},{1,17},{2,18},{3,19},{4,20},{5,21},{6,22},{7,23},{8,24},{9,... | collective-permute-start | bytes 786440 | tf_op jit(solution)/shard_map/ppermute | solution.py:74
  17.5 65.5 %collective-permute-start.17 = (bf16[2,256,2,128]{1,3,2,0:T(8,128)(2,1)}, bf16[2,256,2,128]{1,3,2,0:T(8,128)(2,1)}, u32[]{:S(2)}, u32[]{:S(2)}) collective-permute-start(bf16[2,256,2,128]{1,3,2,0:T(8,128)(2,1)} %get-tuple-element.108), channel_id=1, source_target_pairs={{112,127},{113,126},{114,125},{115,124},{116,123},{117,122},{118,1... | collective-permute-start | bytes 786440 | tf_op jit(solution)/shard_map/ppermute | solution.py:78
  18.8 62.7 %collective-permute-start.16 = (bf16[2,256,2,128]{1,3,2,0:T(8,128)(2,1)}, bf16[2,256,2,128]{1,3,2,0:T(8,128)(2,1)}, u32[]{:S(2)}, u32[]{:S(2)}) collective-permute-start(bf16[2,256,2,128]{1,3,2,0:T(8,128)(2,1)} %get-tuple-element.107), channel_id=1, source_target_pairs={{16,0},{17,1},{18,2},{19,3},{20,4},{21,5},{22,6},{23,7},{24,8},{25... | collective-permute-start | bytes 786440 | tf_op jit(solution)/shard_map/ppermute | solution.py:75
  20.1 64.7 %collective-permute-start.18 = (bf16[2,256,2,128]{1,3,2,0:T(8,128)(2,1)}, bf16[2,256,2,128]{1,3,2,0:T(8,128)(2,1)}, u32[]{:S(2)}, u32[]{:S(2)}) collective-permute-start(bf16[2,256,2,128]{1,3,2,0:T(8,128)(2,1)} %get-tuple-element.107), channel_id=1, source_target_pairs={{15,0},{16,1},{17,2},{18,3},{19,4},{20,5},{21,6},{22,7},{23,8},{24... | collective-permute-start | bytes 786440 | tf_op jit(solution)/shard_map/ppermute | solution.py:75
  21.4 64.7 %collective-permute-start.19 = (bf16[2,256,2,128]{1,3,2,0:T(8,128)(2,1)}, bf16[2,256,2,128]{1,3,2,0:T(8,128)(2,1)}, u32[]{:S(2)}, u32[]{:S(2)}) collective-permute-start(bf16[2,256,2,128]{1,3,2,0:T(8,128)(2,1)} %get-tuple-element.108), channel_id=1, source_target_pairs={{113,127},{114,126},{115,125},{116,124},{117,123},{118,122},{119,1... | collective-permute-start | bytes 786440 | tf_op jit(solution)/shard_map/ppermute | solution.py:78
  121.3 54.3 %collective-permute-start.33 = (bf16[2,256,2,128]{1,3,2,0:T(8,128)(2,1)}, bf16[2,256,2,128]{1,3,2,0:T(8,128)(2,1)S(1)}, u32[]{:S(2)}, u32[]{:S(2)}) collective-permute-start(bf16[2,256,2,128]{1,3,2,0:T(8,128)(2,1)} %get-tuple-element.108), channel_id=1, source_target_pairs={{120,127},{121,126},{122,125},{123,124},{124,123},{125,122},{126,1... | collective-permute-start | bytes 786440 | tf_op jit(solution)/shard_map/ppermute | solution.py:78
  125.5 50.9 %collective-permute-start.34 = (bf16[2,256,2,128]{1,3,2,0:T(8,128)(2,1)}, bf16[2,256,2,128]{1,3,2,0:T(8,128)(2,1)S(1)}, u32[]{:S(2)}, u32[]{:S(2)}) collective-permute-start(bf16[2,256,2,128]{1,3,2,0:T(8,128)(2,1)} %get-tuple-element.107), channel_id=1, source_target_pairs={{7,0},{8,1},{9,2},{10,3},{11,4},{12,5},{13,6},{14,7},{15,8},{16,9}... | collective-permute-start | bytes 786440 | tf_op jit(solution)/shard_map/ppermute | solution.py:75
  126.8 61.7 %collective-permute-start.35 = (bf16[2,256,2,128]{1,3,2,0:T(8,128)(2,1)}, bf16[2,256,2,128]{1,3,2,0:T(8,128)(2,1)S(1)}, u32[]{:S(2)}, u32[]{:S(2)}) collective-permute-start(bf16[2,256,2,128]{1,3,2,0:T(8,128)(2,1)} %get-tuple-element.108), channel_id=1, source_target_pairs={{121,127},{122,126},{123,125},{125,123},{126,122},{127,121}} | collective-permute-start | bytes 786440 | tf_op jit(solution)/shard_map/ppermute | solution.py:78
  134.1 55.2 %collective-permute-start.36 = (bf16[2,256,2,128]{1,3,2,0:T(8,128)(2,1)}, bf16[2,256,2,128]{1,3,2,0:T(8,128)(2,1)S(1)}, u32[]{:S(2)}, u32[]{:S(2)}) collective-permute-start(bf16[2,256,2,128]{1,3,2,0:T(8,128)(2,1)} %get-tuple-element.107), channel_id=1, source_target_pairs={{6,0},{7,1},{8,2},{9,3},{10,4},{11,5},{12,6},{13,7},{14,8},{15,9},... | collective-permute-start | bytes 786440 | tf_op jit(solution)/shard_map/ppermute | solution.py:75
  188.5 26.1 %collective-permute-start.39 = (bf16[2,256,2,128]{1,3,2,0:T(8,128)(2,1)}, bf16[2,256,2,128]{1,3,2,0:T(8,128)(2,1)S(1)}, u32[]{:S(2)}, u32[]{:S(2)}) collective-permute-start(bf16[2,256,2,128]{1,3,2,0:T(8,128)(2,1)} %get-tuple-element.108), channel_id=1, source_target_pairs={{123,127},{124,126},{126,124},{127,123}} | collective-permute-start | bytes 786440 | tf_op jit(solution)/shard_map/ppermute | solution.py:78
  215.4 30.9 %collective-permute-start.1 = (bf16[2,256,2,128]{1,3,2,0:T(8,128)(2,1)}, bf16[2,256,2,128]{1,3,2,0:T(8,128)(2,1)S(1)}, u32[]{:S(2)}, u32[]{:S(2)}) collective-permute-start(bf16[2,256,2,128]{1,3,2,0:T(8,128)(2,1)} %get-tuple-element.108), channel_id=1, source_target_pairs={{0,15},{1,16},{2,17},{3,18},{4,19},{5,20},{6,21},{7,22},{8,23},{9,... | collective-permute-start | bytes 786440 | tf_op jit(solution)/shard_map/ppermute | solution.py:74
  221.2 26.5 %collective-permute-start.2 = (bf16[2,256,2,128]{1,3,2,0:T(8,128)(2,1)}, bf16[2,256,2,128]{1,3,2,0:T(8,128)(2,1)S(1)}, u32[]{:S(2)}, u32[]{:S(2)}) collective-permute-start(bf16[2,256,2,128]{1,3,2,0:T(8,128)(2,1)} %get-tuple-element.108), channel_id=1, source_target_pairs={{0,14},{1,15},{2,16},{3,17},{4,18},{5,19},{6,20},{7,21},{8,22},{9,... | collective-permute-start | bytes 786440 | tf_op jit(solution)/shard_map/ppermute | solution.py:74
  225.7 38.8 %collective-permute-start.3 = (bf16[2,256,2,128]{1,3,2,0:T(8,128)(2,1)}, bf16[2,256,2,128]{1,3,2,0:T(8,128)(2,1)S(1)}, u32[]{:S(2)}, u32[]{:S(2)}) collective-permute-start(bf16[2,256,2,128]{1,3,2,0:T(8,128)(2,1)} %get-tuple-element.108), channel_id=1, source_target_pairs={{0,13},{1,14},{2,15},{3,16},{4,17},{5,18},{6,19},{7,20},{8,21},{9,... | collective-permute-start | bytes 786440 | tf_op jit(solution)/shard_map/ppermute | solution.py:74
  230.4 35.5 %collective-permute-start.4 = (bf16[2,256,2,128]{1,3,2,0:T(8,128)(2,1)}, bf16[2,256,2,128]{1,3,2,0:T(8,128)(2,1)S(1)}, u32[]{:S(2)}, u32[]{:S(2)}) collective-permute-start(bf16[2,256,2,128]{1,3,2,0:T(8,128)(2,1)} %get-tuple-element.108), channel_id=1, source_target_pairs={{0,12},{1,13},{2,14},{3,15},{4,16},{5,17},{6,18},{7,19},{8,20},{9,... | collective-permute-start | bytes 786440 | tf_op jit(solution)/shard_map/ppermute | solution.py:74
  235.8 31.4 %collective-permute-start.5 = (bf16[2,256,2,128]{1,3,2,0:T(8,128)(2,1)}, bf16[2,256,2,128]{1,3,2,0:T(8,128)(2,1)S(1)}, u32[]{:S(2)}, u32[]{:S(2)}) collective-permute-start(bf16[2,256,2,128]{1,3,2,0:T(8,128)(2,1)} %get-tuple-element.108), channel_id=1, source_target_pairs={{0,11},{1,12},{2,13},{3,14},{4,15},{5,16},{6,17},{7,18},{8,19},{9,... | collective-permute-start | bytes 786440 | tf_op jit(solution)/shard_map/ppermute | solution.py:74
  247.7 38.6 %collective-permute-start.7 = (bf16[2,256,2,128]{1,3,2,0:T(8,128)(2,1)}, bf16[2,256,2,128]{1,3,2,0:T(8,128)(2,1)S(1)}, u32[]{:S(2)}, u32[]{:S(2)}) collective-permute-start(bf16[2,256,2,128]{1,3,2,0:T(8,128)(2,1)} %get-tuple-element.108), channel_id=1, source_target_pairs={{0,9},{1,10},{2,11},{3,12},{4,13},{5,14},{6,15},{7,16},{8,17},{9,1... | collective-permute-start | bytes 786440 | tf_op jit(solution)/shard_map/ppermute | solution.py:74
  264.5 32.0 %collective-permute-start.8 = (bf16[2,256,2,128]{1,3,2,0:T(8,128)(2,1)}, bf16[2,256,2,128]{1,3,2,0:T(8,128)(2,1)S(1)}, u32[]{:S(2)}, u32[]{:S(2)}) collective-permute-start(bf16[2,256,2,128]{1,3,2,0:T(8,128)(2,1)} %get-tuple-element.108), channel_id=1, source_target_pairs={{0,8},{1,9},{2,10},{3,11},{4,12},{5,13},{6,14},{7,15},{8,16},{9,17... | collective-permute-start | bytes 786440 | tf_op jit(solution)/shard_map/ppermute | solution.py:74
  265.9 40.9 %collective-permute-start.9 = (bf16[2,256,2,128]{1,3,2,0:T(8,128)(2,1)}, bf16[2,256,2,128]{1,3,2,0:T(8,128)(2,1)S(1)}, u32[]{:S(2)}, u32[]{:S(2)}) collective-permute-start(bf16[2,256,2,128]{1,3,2,0:T(8,128)(2,1)} %get-tuple-element.108), channel_id=1, source_target_pairs={{0,7},{1,8},{2,9},{3,10},{4,11},{5,12},{6,13},{7,14},{8,15},{9,16}... | collective-permute-start | bytes 786440 | tf_op jit(solution)/shard_map/ppermute | solution.py:74
  267.2 49.7 %collective-permute-start.10 = (bf16[2,256,2,128]{1,3,2,0:T(8,128)(2,1)}, bf16[2,256,2,128]{1,3,2,0:T(8,128)(2,1)S(1)}, u32[]{:S(2)}, u32[]{:S(2)}) collective-permute-start(bf16[2,256,2,128]{1,3,2,0:T(8,128)(2,1)} %get-tuple-element.108), channel_id=1, source_target_pairs={{0,6},{1,7},{2,8},{3,9},{4,10},{5,11},{6,12},{7,13},{8,14},{9,15},... | collective-permute-start | bytes 786440 | tf_op jit(solution)/shard_map/ppermute | solution.py:74
  269.0 58.1 %collective-permute-start.11 = (bf16[2,256,2,128]{1,3,2,0:T(8,128)(2,1)}, bf16[2,256,2,128]{1,3,2,0:T(8,128)(2,1)S(1)}, u32[]{:S(2)}, u32[]{:S(2)}) collective-permute-start(bf16[2,256,2,128]{1,3,2,0:T(8,128)(2,1)} %get-tuple-element.108), channel_id=1, source_target_pairs={{0,5},{1,6},{2,7},{3,8},{4,9},{5,10},{6,11},{7,12},{8,13},{9,14},{... | collective-permute-start | bytes 786440 | tf_op jit(solution)/shard_map/ppermute | solution.py:74
  286.3 50.5 %collective-permute-start.12 = (bf16[2,256,2,128]{1,3,2,0:T(8,128)(2,1)}, bf16[2,256,2,128]{1,3,2,0:T(8,128)(2,1)S(1)}, u32[]{:S(2)}, u32[]{:S(2)}) collective-permute-start(bf16[2,256,2,128]{1,3,2,0:T(8,128)(2,1)} %get-tuple-element.108), channel_id=1, source_target_pairs={{0,4},{1,5},{2,6},{3,7},{4,8},{5,9},{6,10},{7,11},{8,12},{9,13},{1... | collective-permute-start | bytes 786440 | tf_op jit(solution)/shard_map/ppermute | solution.py:74
  296.5 40.9 %collective-permute-start.13 = (bf16[2,256,2,128]{1,3,2,0:T(8,128)(2,1)}, bf16[2,256,2,128]{1,3,2,0:T(8,128)(2,1)S(1)}, u32[]{:S(2)}, u32[]{:S(2)}) collective-permute-start(bf16[2,256,2,128]{1,3,2,0:T(8,128)(2,1)} %get-tuple-element.108), channel_id=1, source_target_pairs={{0,3},{1,4},{2,5},{3,6},{4,7},{5,8},{6,9},{7,10},{8,11},{9,12},{10... | collective-permute-start | bytes 786440 | tf_op jit(solution)/shard_map/ppermute | solution.py:74
  306.7 42.4 %collective-permute-start.14 = (bf16[2,256,2,128]{1,3,2,0:T(8,128)(2,1)}, bf16[2,256,2,128]{1,3,2,0:T(8,128)(2,1)S(1)}, u32[]{:S(2)}, u32[]{:S(2)}) collective-permute-start(bf16[2,256,2,128]{1,3,2,0:T(8,128)(2,1)} %get-tuple-element.108), channel_id=1, source_target_pairs={{0,2},{1,3},{2,4},{3,5},{4,6},{5,7},{6,8},{7,9},{8,10},{9,11},{10,... | collective-permute-start | bytes 786440 | tf_op jit(solution)/shard_map/ppermute | solution.py:74
  317.0 32.3 %collective-permute-start.15 = (bf16[2,256,2,128]{1,3,2,0:T(8,128)(2,1)}, bf16[2,256,2,128]{1,3,2,0:T(8,128)(2,1)S(1)}, u32[]{:S(2)}, u32[]{:S(2)}) collective-permute-start(bf16[2,256,2,128]{1,3,2,0:T(8,128)(2,1)} %get-tuple-element.108), channel_id=1, source_target_pairs={{0,1},{1,2},{2,3},{3,4},{4,5},{5,6},{6,7},{7,8},{8,9},{9,10},{10,1... | collective-permute-start | bytes 786440 | tf_op jit(solution)/shard_map/ppermute | solution.py:74
  (28 other events, 416.9 us)
where the time goes:
time: 601 us; the launch traced here: 599 us
  starting transfers between devices  235 us (39%)
  matrix products  181 us (30%)
  other arithmetic  87.6 us (15%)
  local copies, waits for them, and re-layouts  48.4 us (8%)
  waiting for transfers between devices  44.2 us (7%)
    ppermute x16, starting transfers between devices, device_step(): lax.ppermute(kv_second, 'cp', [(sender, sender - offset) for sender in ra...  112 us
    ppermute x16, starting transfers between devices, device_step(): lax.ppermute(kv_first, 'cp', [(sender, sender + offset) for sender in ran...  111 us
    dot_general x2, matrix products, one_block(): jnp.einsum('nqkgd,nskd->nkgqs', q_part, k_part, preferred_element_type=jn...  76.7 us
    dot_general x2, matrix products, one_block(): jnp.einsum('nkgqs,nskd->nqkgd', exp_scores.astype(jnp.bfloat16), v_part,...  72.3 us
    reduce_sum x2, other arithmetic, one_block(): row_sum = jnp.sum(exp_scores, axis=-1)  64.1 us
    ppermute x16, waiting for transfers between devices, device_step(): lax.ppermute(kv_second, 'cp', [(sender, sender - offset) for sender in ra...  39 us
    unnamed x28, local copies, waits for them, and re-layouts  31.4 us
    dot_general x1, matrix products, device_step(): jnp.einsum('nqkge,kgem->nqm', attended, w_out, preferred_element_type=jnp...  14.8 us
  transfers between devices with their start and end apart: 47, of which 9 were waited for; matrix products, arithmetic and copies ran while one was open for 11% of the time, Pallas kernels for 0%

commit v1 on v0

v1 whole, which is shorter than its diff:
```python
import functools

import jax
import jax.numpy as jnp
from jax import lax
from jax.experimental import pallas as pl
from jax.experimental.pallas import tpu as pltpu
from jax.sharding import PartitionSpec as P

WINDOW = 4096
ROPE_BASE = 10000.0
CHUNK = 256
REACH = WINDOW // CHUNK
GROUP = 4
STEPS = REACH // GROUP
HEADS = 24
KV_HEADS = 2
SHARE = HEADS // KV_HEADS
DIM = 128
NEG = -1e30
MESH = pl.DeviceIdType.MESH

OFFSETS = (16, 2, 1, 4, 3, 6, 5, 8, 7, 10, 9, 12, 11, 14, 13, 15)
SLOT = {offset: slot for slot, offset in enumerate(OFFSETS)}
NEAR = (8, 1, 2, 3, 4, 5, 6, 7)


def rotation(positions):
    inv_freq = 1.0 / (ROPE_BASE ** (jnp.arange(DIM // 2, dtype=jnp.float32) * (2.0 / DIM)))
    angles = positions.astype(jnp.float32)[..., None, None] * inv_freq
    return jnp.cos(angles), jnp.sin(angles)


def rotate(values, cos_part, sin_part, factor):
    first = values[..., : DIM // 2].astype(jnp.float32)
    second = values[..., DIM // 2 :].astype(jnp.float32)
    rotated = jnp.concatenate([first * cos_part - second * sin_part, second * cos_part + first * sin_part], axis=-1)
    return (rotated * factor).astype(jnp.bfloat16)


def fold8(values, op):
    return op(values.reshape(values.shape[0] // 8, 8, values.shape[1]), axis=0)


def attention_kernel(cp, q_ref, k_ref, v_ref, o_ref, kbuf, vbuf, s_a, s_b, p_a, p_b, x_a, x_b, al_a, al_b, acc, mrun, lrun, send_sem, fwd_sem, recv_sem):
    me = lax.axis_index("cp")
    chunk_of = (me, 2 * cp - 1 - me)
    even_of = (lax.rem(me, 2) == 0, lax.rem(me, 2) == 1)
    partner = me + 1 - 2 * lax.rem(me, 2)

    def direct(role, t):
        if role == 0:
            there = me + 2 * t
            low = there < cp
            return None, jnp.where(low, there, 2 * cp - 1 - there), jnp.where(low, 0, 1)
        return me >= 2 * t, me - 2 * t, 1

    def copies(src_k, src_v, band, slot, sems, device):
        for kind, (src, dst) in enumerate(((src_k, kbuf), (src_v, vbuf))):
            yield pltpu.make_async_remote_copy(
                src_ref=src, dst_ref=dst.at[band, :, slot], send_sem=sems.at[kind], recv_sem=recv_sem.at[band, slot, kind],
                device_id={"cp": device}, device_id_type=MESH)

    def when(cond, fn):
        if cond is None:
            fn()
        else:
            pl.when(cond)(fn)

    for slot, offset in enumerate(OFFSETS):
        @pl.when(me < offset)
        def _(slot=slot):
            kbuf[0, :, slot] = jnp.zeros((KV_HEADS, CHUNK, DIM), jnp.bfloat16)
            vbuf[0, :, slot] = jnp.zeros((KV_HEADS, DIM, CHUNK), jnp.bfloat16)

    barrier = pltpu.get_barrier_semaphore()
    pl.semaphore_signal(barrier, inc=1, device_id={"cp": partner}, device_id_type=MESH)
    for role in range(2):
        for t in NEAR:
            runs, device, _ = direct(role, t)
            when(runs, lambda device=device: pl.semaphore_signal(barrier, inc=1, device_id={"cp": device}, device_id_type=MESH))
    pl.semaphore_wait(barrier, 1 + len(NEAR) + jnp.minimum(len(NEAR), me // 2))

    for t in NEAR:
        for role in range(2):
            runs, device, band = direct(role, t)

            def send(role=role, t=t, device=device, band=band):
                for copy in copies(k_ref.at[role], v_ref.at[role], band, SLOT[2 * t], send_sem.at[role, t - 1], device):
                    copy.start()
            when(runs, send)

    def forward_copies(role, e):
        even = even_of[role]
        slot = jnp.where(even, SLOT[min(e + 1, REACH - 1)], SLOT[max(e - 1, 1)])
        src = (k_ref.at[role], v_ref.at[role]) if e == 0 else (kbuf.at[role, :, SLOT[e]], vbuf.at[role, :, SLOT[e]])
        return copies(*src, role, slot, fwd_sem.at[role, e // 2], partner)

    def forwards(role, e):
        even = even_of[role]
        mine = even if e == 0 else (jnp.logical_not(even) if e == REACH else None)
        if role == 0 and e > 0:
            there = me >= e
            return there if mine is None else jnp.logical_and(mine, there)
        return mine

    def wait_slot(role, slot):
        def wait():
            for copy in copies(k_ref.at[role], v_ref.at[role], role, slot, send_sem.at[role, 0], partner):
                copy.wait_recv()
        when(None if role else me >= OFFSETS[slot], wait)

    def receive_direct(role, group):
        for slot in range(GROUP * group, GROUP * group + GROUP):
            e = OFFSETS[slot]
            if e % 2 == 0:
                wait_slot(role, slot)

                def push(e=e):
                    for copy in forward_copies(role, e):
                        copy.start()
                when(forwards(role, e), push)

    def receive_forwarded(role, group):
        for slot in range(GROUP * group, GROUP * group + GROUP):
            if OFFSETS[slot] % 2:
                wait_slot(role, slot)

    for role in range(2):
        def push(role=role):
            for copy in forward_copies(role, 0):
                copy.start()
        when(forwards(role, 0), push)

    key_ids = lax.broadcasted_iota(jnp.int32, (CHUNK, CHUNK), 0)
    query_ids = lax.broadcasted_iota(jnp.int32, (CHUNK, CHUNK), 1)

    def query(role, h):
        return q_ref[pl.ds(pl.multiple_of(role * CHUNK, CHUNK), CHUNK), pl.ds(pl.multiple_of(h * DIM, DIM), DIM)]

    def scores(keys, qh):
        return lax.dot_general(keys, qh, (((1,), (1,)), ((), ())), preferred_element_type=jnp.float32)

    def bias_of(role, slot, offset):
        return jnp.where(jnp.logical_and(role == 0, me < offset), jnp.float32(NEG), jnp.float32(0))

    def offset_of(slot):
        odd = lax.rem(slot, 2)
        return jnp.where(slot == REACH - 1, REACH - 1, jnp.where(odd == 1, slot + 1, slot - 1))

    def stage_qk(role, group, h, s_ref, x_ref, first):
        kv = h // SHARE
        qh = query(role, h)
        top = None
        for c in range(GROUP):
            slot = GROUP * group + c
            s = scores(kbuf[role, kv, slot], qh)
            if first and c == 0:
                own = scores(k_ref[role, kv], qh)
                s = jnp.where(key_ids <= query_ids, own, s + bias_of(role, slot, REACH))
                part = fold8(s, jnp.max)
            else:
                offset = OFFSETS[c] if first else offset_of(slot)
                part = fold8(s, jnp.max) + bias_of(role, slot, offset)
            s_ref[pl.ds(c * CHUNK, CHUNK), :] = s
            top = part if top is None else jnp.maximum(top, part)
        x_ref[...] = top

    def stage_softmax(role, group, h, s_ref, x_ref, p_ref, al_ref, first):
        row = role * HEADS + h
        top = jnp.max(x_ref[...], axis=0, keepdims=True)
        if first:
            m = top
        else:
            old = mrun[row, 0:1]
            m = jnp.maximum(old, top)
            alpha = jnp.exp(old - m)
            al_ref[...] = jnp.broadcast_to(alpha, (8, CHUNK))
        mrun[row] = jnp.broadcast_to(m, (8, CHUNK))
        total = None
        for c in range(GROUP):
            slot = GROUP * group + c
            if first and c == 0:
                shift = m
            else:
                shift = m - bias_of(role, slot, OFFSETS[c] if first else offset_of(slot))
            e = jnp.exp(s_ref[pl.ds(c * CHUNK, CHUNK), :] - shift)
            part = fold8(e, jnp.sum)
            total = part if total is None else total + part
            p_ref[pl.ds(c * CHUNK, CHUNK), :] = e.astype(jnp.bfloat16)
        lrun[row] = total if first else lrun[row] * alpha + total

    def stage_pv(role, group, h, row, p_ref, al_ref, first):
        kv = h // SHARE
        out = None
        for c in range(GROUP):
            slot = GROUP * group + c
            p = p_ref[pl.ds(c * CHUNK, CHUNK), :]
            values = vbuf[role, kv, slot]
            if first and c == 0:
                causal = key_ids <= query_ids
                none = jnp.zeros_like(p)
                part = jnp.dot(v_ref[role, kv], jnp.where(causal, p, none), preferred_element_type=jnp.float32)
                part += jnp.dot(values, jnp.where(causal, none, p), preferred_element_type=jnp.float32)
            else:
                part = jnp.dot(values, p, preferred_element_type=jnp.float32)
            out = part if out is None else out + part
        if first:
            acc[row] = out
        else:
            acc[row] = acc[row] * al_ref[0:1] + out

    HALF = HEADS // 2

    def run(first_step, n_steps, first, receive):
        n_units = n_steps * HEADS

        def place(unit):
            step = first_step + unit // HEADS
            return lax.rem(step, 2), step // 2, lax.rem(unit, HEADS)

        def qk(unit, s_ref, x_ref):
            stage_qk(*place(unit), s_ref, x_ref, first)

        def softmax(unit, *refs):
            stage_softmax(*place(unit), *refs, first)

        def pv(unit, row, *refs):
            role, group, h = place(unit)
            stage_pv(role, group, h, row, *refs, first)

        def row_of(unit):
            role, _, h = place(unit)
            return role * HEADS + h

        qk(0, s_a, x_a)

        def body(i, carry):
            receive(i)
            unit = 2 * i
            before = jnp.maximum(unit - 1, 0)
            after = jnp.minimum(unit + 2, n_units - 1)
            qk(unit + 1, s_b, x_b)
            softmax(unit, s_a, x_a, p_a, al_a)
            pv(before, jnp.where(i == 0, 2 * HEADS, row_of(before)), p_b, al_b)
            qk(after, s_a, x_a)
            softmax(unit + 1, s_b, x_b, p_b, al_b)
            pv(unit, row_of(unit), p_a, al_a)
            return carry

        lax.fori_loop(0, n_units // 2, body, 0)
        pv(n_units - 1, row_of(n_units - 1), p_b, al_b)

    receive_direct(0, 0)
    receive_direct(1, 0)
    receive_forwarded(0, 0)

    def receive_first(i):
        @pl.when(i == HALF - 2)
        def _():
            receive_forwarded(1, 0)

    def receive_rest(i):
        for step in range(2 * STEPS - 3):
            @pl.when(i == HALF * step + HALF - 2)
            def _(step=step):
                group, role = divmod(step + 3, 2)
                if step + 4 < 2 * STEPS:
                    ahead, other = divmod(step + 4, 2)
                    receive_direct(other, ahead)
                receive_forwarded(role, group)

    p_b[...] = jnp.zeros_like(p_b)
    al_b[...] = jnp.zeros_like(al_b)
    acc[2 * HEADS] = jnp.zeros((DIM, CHUNK), jnp.float32)
    run(0, 2, True, receive_first)
    receive_direct(0, 1)
    receive_direct(1, 1)
    receive_forwarded(0, 1)
    run(2, 2 * STEPS - 2, False, receive_rest)

    def finish(j, carry):
        for k in range(2):
            row = 2 * j + k
            total = jnp.sum(lrun[row], axis=0, keepdims=True)
            out = (acc[row] * (1.0 / total)).astype(jnp.bfloat16)
            role, h = row // HEADS, lax.rem(row, HEADS)
            o_ref[pl.ds(pl.multiple_of(role * CHUNK, CHUNK), CHUNK), pl.ds(pl.multiple_of(h * DIM, DIM), DIM)] = out.T
        return carry

    lax.fori_loop(0, HEADS, finish, 0)

    for t in NEAR:
        for role in range(2):
            runs, device, band = direct(role, t)

            def drain(role=role, t=t, device=device, band=band):
                for copy in copies(k_ref.at[role], v_ref.at[role], band, SLOT[2 * t], send_sem.at[role, t - 1], device):
                    copy.wait_send()
            when(runs, drain)
    for role in range(2):
        for e in range(0, REACH + 1, 2):
            def drain(role=role, e=e):
                for copy in forward_copies(role, e):
                    copy.wait_send()
            when(forwards(role, e), drain)


def attend(cp, queries, keys, values):
    f32, bf16 = jnp.float32, jnp.bfloat16
    vmem = pl.BlockSpec(memory_space=pltpu.VMEM)
    return pl.pallas_call(
        functools.partial(attention_kernel, cp),
        name="band_attention",
        out_shape=jax.ShapeDtypeStruct(queries.shape, bf16),
        in_specs=[vmem] * 3,
        out_specs=vmem,
        scratch_shapes=[
            pltpu.VMEM((2, KV_HEADS, REACH, CHUNK, DIM), bf16),
            pltpu.VMEM((2, KV_HEADS, REACH, DIM, CHUNK), bf16),
            pltpu.VMEM((GROUP * CHUNK, CHUNK), f32),
            pltpu.VMEM((GROUP * CHUNK, CHUNK), f32),
            pltpu.VMEM((GROUP * CHUNK, CHUNK), bf16),
            pltpu.VMEM((GROUP * CHUNK, CHUNK), bf16),
            pltpu.VMEM((8, CHUNK), f32),
            pltpu.VMEM((8, CHUNK), f32),
            pltpu.VMEM((8, CHUNK), f32),
            pltpu.VMEM((8, CHUNK), f32),
            pltpu.VMEM((2 * HEADS + 1, DIM, CHUNK), f32),
            pltpu.VMEM((2 * HEADS, 8, CHUNK), f32),
            pltpu.VMEM((2 * HEADS, 8, CHUNK), f32),
            pltpu.SemaphoreType.DMA((2, len(NEAR), 2)),
            pltpu.SemaphoreType.DMA((2, REACH // 2 + 1, 2)),
            pltpu.SemaphoreType.DMA((2, REACH, 2)),
        ],
        compiler_params=pltpu.CompilerParams(collective_id=0, has_side_effects=True, vmem_limit_bytes=60 * 1024 * 1024),
    )(queries, keys, values)


def solution(mesh):
    cp = mesh.shape["cp"]

    def device_step(hidden, w_q, w_k, w_v, w_o):
        me = lax.axis_index("cp")
        model_dim = hidden.shape[1]
        x = hidden.reshape(2, CHUNK, model_dim)
        chunk_ids = jnp.stack([me, 2 * cp - 1 - me])
        positions = chunk_ids[:, None] * CHUNK + jnp.arange(CHUNK)[None, :]
        cos_part, sin_part = rotation(positions)
        k_proj = jnp.einsum("nqd,dhe->nqhe", x, w_k, preferred_element_type=jnp.float32).astype(jnp.bfloat16)
        v_proj = jnp.einsum("nqd,dhe->nheq", x, w_v, preferred_element_type=jnp.float32).astype(jnp.bfloat16)
        keys = jnp.transpose(rotate(k_proj, cos_part, sin_part, 1.0), (0, 2, 1, 3))
        q_proj = jnp.einsum("nqd,dhe->nqhe", x, w_q, preferred_element_type=jnp.float32).astype(jnp.bfloat16)
        queries = rotate(q_proj, cos_part, sin_part, DIM ** -0.5).reshape(2 * CHUNK, HEADS * DIM)
        attended = attend(cp, queries, keys, v_proj)
        out = jnp.dot(attended, w_o.reshape(HEADS * DIM, model_dim), preferred_element_type=jnp.float32)
        return out.astype(jnp.bfloat16)

    return jax.shard_map(device_step, mesh=mesh, in_specs=(P(("dp", "cp"), None), P(), P(), P(), P()), out_specs=P(("dp", "cp"), None), check_vma=False)
```

time: 601 us -> 219 us (0.36)
  starting transfers between devices: 235 us -> 0 us
  matrix products: 181 us -> 35.5 us
  Pallas kernels: 0 us -> 137 us
  other arithmetic: 87.6 us -> 6.6 us
  waiting for transfers between devices: 44.2 us -> 0 us
  local copies, waits for them, and re-layouts: 48.4 us -> 38.8 us
    ppermute x47 -> x0, starting transfers between devices: 235 us -> none  [the longest x16 112 us: device_step(): lax.ppermute(kv_second, 'cp', [(sender, sender - offset) for sender in ra...]
    dot_general x8 -> x4, matrix products: 181 us -> 35.5 us  [the longest x1 16 us: device_step(): jnp.dot(attended, w_o.reshape(HEADS * DIM, model_dim), preferred_element_...]
    pallas_call x0 -> x1, Pallas kernels: none -> 137 us  [attend(): pl.pallas_call(functools.partial(attention_kernel, cp), name='band_attent...]
    reduce_sum x2 -> x0, other arithmetic: 64.1 us -> none  [one_block(): row_sum = jnp.sum(exp_scores, axis=-1)]
    ppermute x47 -> x0, waiting for transfers between devices: 44.2 us -> none  [the longest x16 39 us: device_step(): lax.ppermute(kv_second, 'cp', [(sender, sender - offset) for sender in ra...]
    concatenate x3 -> x0, local copies, waits for them, and re-layouts: 9.86 us -> none  [the longest x2 9.82 us: rotate(): jnp.concatenate([first_half * cos_part - second_half * sin_part, second_h...]
    unnamed x28 -> x11, local copies, waits for them, and re-layouts: 31.4 us -> 33.4 us
  transfers between devices with their start and end apart: 47 -> 0, of which waited for: 9 -> 0; matrix products, arithmetic and copies ran while one was open for 11% -> 0% of each run, Pallas kernels for 0% -> 0%
where the time goes in v1:
time: 219 us; the launch traced here: 218 us
  Pallas kernels  137 us (63%)
  local copies, waits for them, and re-layouts  38.8 us (18%)
  matrix products  35.5 us (16%)
  other arithmetic  6.6 us (3%)
    pallas_call x1, Pallas kernels, attend(): pl.pallas_call(functools.partial(attention_kernel, cp), name='band_attent...  137 us
    unnamed x11, local copies, waits for them, and re-layouts  33.4 us
    dot_general x1, matrix products, device_step(): jnp.dot(attended, w_o.reshape(HEADS * DIM, model_dim), preferred_element_...  16 us
    dot_general x1, matrix products, device_step(): jnp.einsum('nqd,dhe->nqhe', x, w_q, preferred_element_type=jnp.float32)  14 us

profile of v1, /device:TPU:1, one launch (start us, length us, event | category | flops | bytes accessed | tf_op | source)
XLA Modules:
  0.0 217.8 jit_solution(10418645599038611791)
XLA Ops:
  0.0 0.0 copy-start
  0.0 0.1 add_multiply_fusion
  0.1 1.8 copy-done
  1.9 0.1 add_convert_fusion
  2.0 3.1 %fusion.18.v_ref = bf16[2,2,128,256]{3,2,1,0:T(8,128)(2,1)} fusion(bf16[2,256,3072,1]{2,1,3,0:T(8,128)(2,1)S(1)} %bitcast.35, bf16[3072,2,128,1]{2,1,0,3:T(2,128)(2,1)} %bitcast.39), kind=kOutput, calls=%fused_computation.19 | convolution fusion | flops 805437440 | bytes 4980736 | tf_op jit(solution)/shard_map/nqd,dhe->nheq/dot_general | solution.py:351
  5.1 1.8 multiply_cosine_fusion
  6.9 0.1 copy.7
  7.0 1.7 copy.8
  8.7 4.9 %copy.10 = bf16[3072,2,128]{0,2,1:T(8,128)(2,1)} copy(bf16[3072,2,128]{2,1,0:T(2,128)(2,1)} %param.7) | data formatting | bytes 3145728 | tf_op args[2]
  13.6 2.5 %fusion.15 = bf16[2,256,2,128]{3,1,2,0:T(8,128)(2,1)S(1)} fusion(bf16[2,256,3072,1]{2,1,3,0:T(8,128)(2,1)S(1)} %bitcast.34, bf16[3072,2,128]{0,2,1:T(8,128)(2,1)} %copy.10), kind=kOutput, calls=%fused_computation.18 | convolution fusion | flops 805437440 | bytes 4980736 | tf_op jit(solution)/shard_map/nqd,dhe->nqhe/dot_general | solution.py:350
  16.1 0.0 copy-done.2
  16.1 0.3 fusion.22
  16.4 0.9 maximum_bitcast_fusion.k_ref
  17.2 24.1 %copy.6 = bf16[3072,24,128]{0,2,1:T(8,128)(2,1)} copy(bf16[3072,24,128]{2,1,0:T(8,128)(2,1)} %param.6) | data formatting | bytes 37748736 | tf_op args[1]
  41.3 14.0 %fusion.5 = bf16[2,256,24,128]{1,3,2,0:T(8,128)(2,1)S(1)} fusion(bf16[2,256,3072,1]{2,1,3,0:T(8,128)(2,1)S(1)} %bitcast.33, bf16[3072,24,128]{0,2,1:T(8,128)(2,1)} %copy.6), kind=kOutput, calls=%fused_computation.12 | convolution fusion | flops 9665249280 | bytes 25165824 | tf_op jit(solution)/shard_map/nqd,dhe->nqhe/dot_general | solution.py:353
  55.3 0.0 copy-done.3
  55.3 1.0 fusion.3
  56.3 2.6 %fusion.2 = bf16[2,256,24,128]{1,3,2,0:T(8,128)(2,1)} fusion(f32[2,256,24,64]{1,3,2,0:T(8,128)S(1)} %get-tuple-element.6, f32[2,256,24,64]{1,3,2,0:T(8,128)S(1)} %get-tuple-element.5), kind=kLoop, calls=%fused_computation.3 | loop fusion | flops 4718592 | bytes 9437184 | tf_op jit(solution)/shard_map/convert_element_type | solution.py:38
  58.9 3.6 %copy.9 = bf16[2,256,24,128]{3,2,1,0:T(8,128)(2,1)S(1)} copy(bf16[2,256,24,128]{1,3,2,0:T(8,128)(2,1)} %fusion.2) | data formatting | bytes 6291456 | tf_op jit(solution)/shard_map/convert_element_type | solution.py:38
  62.5 2.5 %copy.23 = bf16[64,8,24,128]{3,1,2,0:T(8,128)(2,1)} copy(bf16[64,8,24,128]{3,2,1,0:T(8,128)(2,1)S(1)} %bitcast.36) | data formatting | bytes 6291456
  65.0 136.8 %band_attention.1 = bf16[512,3072]{1,0:T(8,128)(2,1)} custom-call(bf16[512,3072]{1,0:T(8,128)(2,1)} %bitcast.37, bf16[2,2,256,128]{3,2,1,0:T(8,128)(2,1)} %maximum_bitcast_fusion.k_ref, bf16[2,2,128,256]{3,2,1,0:T(8,128)(2,1)} %fusion.18.v_ref), custom_call_target="tpu_custom_call" | custom-call | tf_op jit(solution)/shard_map/band_attention/pallas_call | solution.py:312
  201.8 0.0 copy-start.1
  201.8 16.0 %convolution_convert_fusion = bf16[512,3072]{1,0:T(8,128)(2,1)} fusion(bf16[512,3072]{1,0:T(8,128)(2,1)} %band_attention.1, bf16[3072,3072]{1,0:T(8,128)(2,1)} %bitcast.38), kind=kOutput, calls=%fused_computation.4 | convolution fusion | flops 9665249280 | bytes 25165824 | tf_op jit(solution)/shard_map/dot_general | solution.py:356
  217.8 0.0 copy-done.1
  (3 shorter events, 0.0 us)
Async XLA Ops:
  0.0 1.9 copy-start
  13.6 2.5 %copy-start.2 = (f32[2,256,64]{2,1,0:T(8,128)S(1)}, f32[2,256,64]{2,1,0:T(8,128)}, u32[]{:S(2)}) copy-start(f32[2,256,64]{2,1,0:T(8,128)} %get-tuple-element.10) | copy-start | bytes 393220
  41.3 14.0 %copy-start.3 = (f32[2,256,64]{1,2,0:T(8,128)S(1)}, f32[2,256,64]{1,2,0:T(8,128)}, u32[]{:S(2)}) copy-start(f32[2,256,64]{1,2,0:T(8,128)} %copy.8) | copy-start | bytes 393220
  201.8 16.0 %copy-start.1 = (bf16[512,3072]{1,0:T(8,128)(2,1)S(1)}, bf16[512,3072]{1,0:T(8,128)(2,1)}, u32[]{:S(2)}) copy-start(bf16[512,3072]{1,0:T(8,128)(2,1)} %param.5) | copy-start | bytes 9437188

commit v2 on v1

v2 whole, which is shorter than its diff:
```python
import functools

import jax
import jax.numpy as jnp
from jax import lax
from jax.experimental import pallas as pl
from jax.experimental.pallas import tpu as pltpu
from jax.sharding import PartitionSpec as P

WINDOW = 4096
ROPE_BASE = 10000.0
CHUNK = 256
REACH = WINDOW // CHUNK
GROUP = 4
STEPS = REACH // GROUP
PAIRS = 1
HEADS = 24
KV_HEADS = 2
SHARE = HEADS // KV_HEADS
DIM = 128
NEG = -1e30
HALF = CHUNK // 2
PIECE = 32
MESH = pl.DeviceIdType.MESH

OFFSETS = (16, 8, 2, 1, 6, 10, 9, 7, 14, 15, 4, 3, 12, 5, 11, 13)
SLOT = {offset: slot for slot, offset in enumerate(OFFSETS)}
ROW = 8
SENDS = 8
HEAD_TILE = 8
K_BLOCK = 768


def rotation(positions):
    inv_freq = 1.0 / (ROPE_BASE ** (jnp.arange(DIM // 2, dtype=jnp.float32) * (2.0 / DIM)))
    angles = positions.astype(jnp.float32)[:, None] * inv_freq
    cos_part, sin_part = jnp.cos(angles), jnp.sin(angles)
    return jnp.concatenate([cos_part, cos_part], axis=1), jnp.concatenate([-sin_part, sin_part], axis=1)


def fold8(values, op):
    return op(values.reshape(values.shape[0] // 8, 8, values.shape[1]), axis=0)


def attention_kernel(cp, x_ref, w_ref, k_ref, v_ref, cos_ref, sin_ref, o_ref, q_ref, w_in, w_a, w_b, kbuf, vbuf, s_a, s_b, p_a, p_b, x_a, x_b, al_a, al_b, acc, mrun, lrun, w_sem, send_sem, fwd_sem, recv_sem):
    me = lax.axis_index("cp")
    even_of = (lax.rem(me, 2) == 0, lax.rem(me, 2) == 1)
    partner = me + 1 - 2 * lax.rem(me, 2)
    x_of = (lax.rem(me // 2, 4), 3 - lax.rem(me // 2, 4))

    model_dim = x_ref.shape[1]
    n_blocks = model_dim // K_BLOCK
    n_tiles = HEADS // HEAD_TILE

    def fetch(tile, block, slot):
        rows = pl.ds(pl.multiple_of(block * K_BLOCK, K_BLOCK), K_BLOCK)
        heads = pl.ds(pl.multiple_of(tile * HEAD_TILE, HEAD_TILE), HEAD_TILE)
        return pltpu.make_async_copy(w_ref.at[rows, heads], w_in.at[slot], w_sem.at[slot])

    for slot in range(n_blocks):
        fetch(0, slot, slot).start()

    def later(role, step):
        if role:
            return me >= step, me - step, 1
        low = me + step < cp
        return None, jnp.where(low, me + step, 2 * cp - 1 - me - step), jnp.where(low, 0, 1)

    def beside(role, right):
        at = x_of[role]
        move = jnp.where(at == 3, -6, 2) if right else jnp.where(at == 0, 6, -2)
        return me - move if role else me + move

    def copies(src, band, slot, sems, device):
        for kind, (ref, dst) in enumerate(zip(src, (kbuf, vbuf))):
            yield pltpu.make_async_remote_copy(
                src_ref=ref, dst_ref=dst.at[band, :, slot], send_sem=sems.at[kind], recv_sem=recv_sem.at[band, slot, kind],
                device_id={"cp": device}, device_id_type=MESH)

    def both(*conds):
        conds = [c for c in conds if c is not None]
        return functools.reduce(jnp.logical_and, conds) if conds else None

    def when(cond, fn):
        if cond is None:
            fn()
        else:
            pl.when(cond)(fn)

    def exists(role, offset):
        return None if role or not offset else me >= offset

    def own(role):
        return k_ref.at[role], v_ref.at[role]

    def held(role, offset):
        return (kbuf.at[role, :, SLOT[offset]], vbuf.at[role, :, SLOT[offset]]) if offset else own(role)

    def row_send(role, index, offset, right, dest, only=None):
        return both(only, exists(role, offset)), held(role, offset), role, dest, send_sem.at[role, index], beside(role, right)

    def plans(role, stage):
        at = x_of[role]
        pick = lambda cond, a, b: jnp.where(cond, SLOT[a], SLOT[b])
        if stage == "start":
            for index, step in ((0, ROW), (1, 2 * ROW)):
                there, device, band = later(role, step)
                yield there, own(role), band, SLOT[step], send_sem.at[role, index], device
            yield row_send(role, 4, 0, True, SLOT[2], at < 3)
            yield row_send(role, 5, 0, False, SLOT[6], at == 0)
            yield forward(role, 0)
        elif stage == 8:
            yield row_send(role, 2, 8, True, pick(at < 3, 10, 2))
            yield row_send(role, 3, 8, False, pick(at > 0, 6, 14))
        elif stage == 16:
            yield row_send(role, 4, 16, True, SLOT[10], at == 3)
            yield row_send(role, 5, 16, False, SLOT[14], at > 0)
        elif stage == 2:
            yield row_send(role, 6, 2, True, SLOT[4], at == 2)
        elif stage == 10:
            yield row_send(role, 6, 10, True, pick(at < 2, 12, 4), at != 2)
        elif stage == 6:
            yield row_send(role, 7, 6, False, pick(at == 0, 12, 4), at != 1)
        elif stage == 14:
            yield row_send(role, 7, 14, False, SLOT[12], at == 1)
        if stage != "start":
            yield forward(role, stage)

    def forward(role, e):
        even = even_of[role]
        slot = jnp.where(even, SLOT[min(e + 1, REACH - 1)], SLOT[max(e - 1, 1)])
        only = even if e == 0 else (jnp.logical_not(even) if e == REACH else None)
        return both(only, exists(role, e)), held(role, e), role, slot, fwd_sem.at[role, e // 2], partner

    def launch(role, stage):
        for cond, src, band, slot, sems, device in plans(role, stage):
            def go(src=src, band=band, slot=slot, sems=sems, device=device):
                for copy in copies(src, band, slot, sems, device):
                    copy.start()
            when(cond, go)

    def settle(role, stage):
        for cond, src, band, slot, sems, device in plans(role, stage):
            def go(src=src, band=band, slot=slot, sems=sems, device=device):
                for copy in copies(src, band, slot, sems, device):
                    copy.wait_send()
            when(cond, go)

    def arrive(role, offset):
        def wait():
            for copy in copies(own(role), role, SLOT[offset], send_sem.at[role, 0], partner):
                copy.wait_recv()
        when(exists(role, offset), wait)

    def relay(*offsets):
        for offset in offsets:
            for role in range(2):
                arrive(role, offset)
                launch(role, offset)

    def receive_forwarded(role, group):
        for slot in range(GROUP * group, GROUP * group + GROUP):
            if OFFSETS[slot] % 2:
                arrive(role, OFFSETS[slot])

    for slot, offset in enumerate(OFFSETS):
        @pl.when(me < offset)
        def _(slot=slot):
            kbuf[0, :, slot] = jnp.zeros((KV_HEADS, CHUNK, DIM), jnp.bfloat16)
            vbuf[0, :, slot] = jnp.zeros((KV_HEADS, 2, DIM, HALF), jnp.bfloat16)

    barrier = pltpu.get_barrier_semaphore()

    def greet(device):
        pl.semaphore_signal(barrier, inc=1, device_id={"cp": device}, device_id_type=MESH)

    greet(partner)
    greet(beside(0, True))
    greet(beside(0, False))
    for role in range(2):
        for step in (ROW, 2 * ROW):
            there, device, _ = later(role, step)
            when(there, lambda device=device: greet(device))
    pl.semaphore_wait(barrier, 5 + jnp.where(me >= ROW, 1, 0) + jnp.where(me >= 2 * ROW, 1, 0))
    for role in range(2):
        launch(role, "start")

    def relayout(tile, block, w_out):
        fetch(tile, block, block).wait()
        rows = pl.ds(pl.multiple_of(block * K_BLOCK, K_BLOCK), K_BLOCK)
        w_out[rows, :] = w_in[block].reshape(K_BLOCK, HEAD_TILE * DIM)

    def project(tile, pair, w_two):
        cols = pl.ds(pl.multiple_of(pair * 2 * DIM, 2 * DIM), 2 * DIM)
        found = jnp.dot(x_ref[...], w_two[:, cols], preferred_element_type=jnp.float32).astype(jnp.bfloat16).astype(jnp.float32)
        for k in range(2):
            q = found[:, k * DIM : k * DIM + DIM]
            q = (q * cos_ref[...] + pltpu.roll(q, DIM // 2, 1) * sin_ref[...]) * jnp.float32(DIM ** -0.5)
            q = q.astype(jnp.bfloat16)
            h = tile * HEAD_TILE + 2 * pair + k
            q_ref[h] = q[:CHUNK]
            q_ref[HEADS + h] = q[CHUNK:]

    w_two = (w_a, w_b)
    for tile in range(n_tiles + 1):
        def body(block, carry, tile=tile):
            if tile < n_tiles:
                relayout(tile, block, w_two[tile % 2])
                if tile + 1 < n_tiles:
                    fetch(tile + 1, block, block).start()
            if tile:
                project(tile - 1, block, w_two[(tile - 1) % 2])
            return carry
        lax.fori_loop(0, n_blocks, body, 0)
        if tile == 1:
            relay(8)
    relay(16, 2, 6)

    key_ids = lax.broadcasted_iota(jnp.int32, (CHUNK, CHUNK), 0)
    query_ids = lax.broadcasted_iota(jnp.int32, (CHUNK, CHUNK), 1)

    def query(role, h):
        return q_ref[role * HEADS + h]

    def scores(keys, qh):
        return lax.dot_general(keys, qh, (((1,), (1,)), ((), ())), preferred_element_type=jnp.float32)

    def bias_of(role, slot, offset):
        return jnp.where(jnp.logical_and(role == 0, me < offset), jnp.float32(NEG), jnp.float32(0))

    def offset_of(group, c):
        return jnp.where(group == 1, OFFSETS[GROUP + c], jnp.where(group == 2, OFFSETS[2 * GROUP + c], OFFSETS[3 * GROUP + c]))

    def stage_qk(role, group, h, s_ref, x_ref, first):
        kv = h // SHARE
        qh = query(role, h)
        top = None
        for c in range(GROUP):
            slot = GROUP * group + c
            s = scores(kbuf[role, kv, slot], qh)
            if first and c == 0:
                own = scores(k_ref[role, kv], qh)
                s = jnp.where(key_ids <= query_ids, own, s + bias_of(role, slot, REACH))
                part = fold8(s, jnp.max)
            else:
                offset = OFFSETS[c] if first else offset_of(group, c)
                part = fold8(s, jnp.max) + bias_of(role, slot, offset)
            s_ref[pl.ds(c * CHUNK, CHUNK), :] = s
            top = part if top is None else jnp.maximum(top, part)
        x_ref[...] = top

    def stage_softmax(role, group, h, s_ref, x_ref, p_ref, al_ref, first):
        row = role * HEADS + h
        top = jnp.max(x_ref[...], axis=0, keepdims=True)
        if first:
            m = top
        else:
            old = mrun[row, 0:1]
            m = jnp.maximum(old, top)
            alpha = jnp.exp(old - m)
            al_ref[...] = jnp.broadcast_to(alpha, (8, CHUNK))
        mrun[row] = jnp.broadcast_to(m, (8, CHUNK))
        sums = [None, None]
        for c in range(GROUP):
            slot = GROUP * group + c
            shift = m
            if not (first and c == 0):
                shift = m - bias_of(role, slot, OFFSETS[c] if first else offset_of(group, c))
            for half in range(2):
                cols = slice(half * HALF, half * HALF + HALF)
                for r in range(c * CHUNK, c * CHUNK + CHUNK, PIECE):
                    e = jnp.exp(s_ref[r : r + PIECE, cols] - shift[:, cols])
                    part = fold8(e, jnp.sum)
                    sums[half] = part if sums[half] is None else sums[half] + part
                    p_ref[half, r : r + PIECE] = e.astype(jnp.bfloat16)
        total = jnp.concatenate(sums, axis=1)
        lrun[row] = total if first else lrun[row] * alpha + total

    def stage_pv(role, group, h, row, p_ref, al_ref, first):
        kv = h // SHARE
        out = None
        for c in range(GROUP):
            slot = GROUP * group + c
            rows = slice(c * CHUNK, c * CHUNK + CHUNK)
            p = jnp.concatenate([p_ref[0, rows], p_ref[1, rows]], axis=1)
            values = jnp.concatenate([vbuf[role, kv, slot, 0], vbuf[role, kv, slot, 1]], axis=1)
            if first and c == 0:
                causal = key_ids <= query_ids
                none = jnp.zeros_like(p)
                own = jnp.concatenate([v_ref[role, kv, 0], v_ref[role, kv, 1]], axis=1)
                part = jnp.dot(own, jnp.where(causal, p, none), preferred_element_type=jnp.float32)
                part += jnp.dot(values, jnp.where(causal, none, p), preferred_element_type=jnp.float32)
            else:
                part = jnp.dot(values, p, preferred_element_type=jnp.float32)
            out = part if out is None else out + part
        if first:
            acc[row] = out
        else:
            acc[row] = acc[row] * al_ref[0:1] + out

    TRIPS = HEADS // (2 * PAIRS)

    def run(first_step, n_steps, first, receive):
        n_units = n_steps * HEADS

        def place(unit):
            step = first_step + unit // HEADS
            return lax.rem(step, 2), step // 2, lax.rem(unit, HEADS)

        def qk(unit, s_ref, x_ref):
            stage_qk(*place(unit), s_ref, x_ref, first)

        def softmax(unit, *refs):
            stage_softmax(*place(unit), *refs, first)

        def pv(unit, row, *refs):
            role, group, h = place(unit)
            stage_pv(role, group, h, row, *refs, first)

        def row_of(unit):
            role, _, h = place(unit)
            return role * HEADS + h

        qk(0, s_a, x_a)

        def body(i, carry):
            receive(i)
            for pair in range(PAIRS):
                unit = 2 * (PAIRS * i + pair)
                before = jnp.maximum(unit - 1, 0) if pair == 0 else unit - 1
                after = jnp.minimum(unit + 2, n_units - 1) if pair == PAIRS - 1 else unit + 2
                row = jnp.where(i == 0, 2 * HEADS, row_of(before)) if pair == 0 else row_of(before)
                qk(unit + 1, s_b, x_b)
                softmax(unit, s_a, x_a, p_a, al_a)
                pv(before, row, p_b, al_b)
                qk(after, s_a, x_a)
                softmax(unit + 1, s_b, x_b, p_b, al_b)
                pv(unit, row_of(unit), p_a, al_a)
            return carry

        lax.fori_loop(0, n_units // (2 * PAIRS), body, 0)
        pv(n_units - 1, row_of(n_units - 1), p_b, al_b)

    receive_forwarded(0, 0)

    def at(trip, i, fn):
        @pl.when(i == trip)
        def _():
            fn()

    def receive_first(i):
        at(TRIPS // 2, i, lambda: relay(10))
        at(TRIPS - 1, i, lambda: receive_forwarded(1, 0))
        at(TRIPS + TRIPS // 4, i, lambda: relay(14))

    def receive_rest(i):
        at(0, i, lambda: relay(4))
        at(TRIPS, i, lambda: relay(12))
        for step in range(2 * STEPS - 3):
            group, role = divmod(step + 3, 2)
            at(TRIPS * step + TRIPS - 1, i, lambda role=role, group=group: receive_forwarded(role, group))

    p_b[...] = jnp.zeros_like(p_b)
    al_b[...] = jnp.zeros_like(al_b)
    acc[2 * HEADS] = jnp.zeros((DIM, CHUNK), jnp.float32)
    run(0, 2, True, receive_first)
    receive_forwarded(0, 1)
    run(2, 2 * STEPS - 2, False, receive_rest)

    def finish(j, carry):
        for k in range(2):
            row = 2 * j + k
            total = jnp.sum(lrun[row], axis=0, keepdims=True)
            out = (acc[row] * (1.0 / total)).astype(jnp.bfloat16)
            role, h = row // HEADS, lax.rem(row, HEADS)
            o_ref[pl.ds(pl.multiple_of(role * CHUNK, CHUNK), CHUNK), pl.ds(pl.multiple_of(h * DIM, DIM), DIM)] = out.T
        return carry

    lax.fori_loop(0, HEADS, finish, 0)

    for role in range(2):
        for stage in ("start", 8, 16, 2, 10, 6, 14, 4, 12):
            settle(role, stage)


def project_kernel(x_ref, wk_ref, wv_ref, cos_ref, sin_ref, k_ref, v_ref):
    def product(w_ref):
        w = w_ref[...].reshape(x_ref.shape[1], KV_HEADS * DIM)
        return jnp.dot(x_ref[...], w, preferred_element_type=jnp.float32).astype(jnp.bfloat16)

    k_all = product(wk_ref).astype(jnp.float32)
    v_all = product(wv_ref)
    for kv in range(KV_HEADS):
        k = k_all[:, kv * DIM : kv * DIM + DIM]
        k = (k * cos_ref[...] + pltpu.roll(k, DIM // 2, 1) * sin_ref[...]).astype(jnp.bfloat16)
        v = v_all[:, kv * DIM : kv * DIM + DIM]
        for n in range(2):
            k_ref[n, kv] = k[n * CHUNK : n * CHUNK + CHUNK]
            for half in range(2):
                start = n * CHUNK + half * HALF
                v_ref[n, kv, half] = v[start : start + HALF].T


def project_kv(x, w_k, w_v, cos_part, sin_part):
    return pl.pallas_call(
        project_kernel,
        name="project_kv",
        out_shape=(
            jax.ShapeDtypeStruct((2, KV_HEADS, CHUNK, DIM), jnp.bfloat16),
            jax.ShapeDtypeStruct((2, KV_HEADS, 2, DIM, HALF), jnp.bfloat16),
        ),
        compiler_params=pltpu.CompilerParams(vmem_limit_bytes=48 * 1024 * 1024),
    )(x, w_k, w_v, cos_part, sin_part)


def attend(cp, x, w_q, keys, values, cos_part, sin_part):
    f32, bf16 = jnp.float32, jnp.bfloat16
    vmem = pl.BlockSpec(memory_space=pltpu.VMEM)
    n_blocks = x.shape[1] // K_BLOCK
    return pl.pallas_call(
        functools.partial(attention_kernel, cp),
        name="band_attention",
        out_shape=jax.ShapeDtypeStruct((2 * CHUNK, HEADS * DIM), bf16),
        in_specs=[vmem, pl.BlockSpec(memory_space=pl.ANY), vmem, vmem, vmem, vmem],
        out_specs=vmem,
        scratch_shapes=[
            pltpu.VMEM((2 * HEADS, CHUNK, DIM), bf16),
            pltpu.VMEM((n_blocks, K_BLOCK, HEAD_TILE, DIM), bf16),
            pltpu.VMEM((x.shape[1], HEAD_TILE * DIM), bf16),
            pltpu.VMEM((x.shape[1], HEAD_TILE * DIM), bf16),
            pltpu.VMEM((2, KV_HEADS, REACH, CHUNK, DIM), bf16),
            pltpu.VMEM((2, KV_HEADS, REACH, 2, DIM, HALF), bf16),
            pltpu.VMEM((GROUP * CHUNK, CHUNK), f32),
            pltpu.VMEM((GROUP * CHUNK, CHUNK), f32),
            pltpu.VMEM((2, GROUP * CHUNK, HALF), bf16),
            pltpu.VMEM((2, GROUP * CHUNK, HALF), bf16),
            pltpu.VMEM((8, CHUNK), f32),
            pltpu.VMEM((8, CHUNK), f32),
            pltpu.VMEM((8, CHUNK), f32),
            pltpu.VMEM((8, CHUNK), f32),
            pltpu.VMEM((2 * HEADS + 1, DIM, CHUNK), f32),
            pltpu.VMEM((2 * HEADS, 8, CHUNK), f32),
            pltpu.VMEM((2 * HEADS, 8, CHUNK), f32),
            pltpu.SemaphoreType.DMA((n_blocks,)),
            pltpu.SemaphoreType.DMA((2, SENDS, 2)),
            pltpu.SemaphoreType.DMA((2, REACH // 2 + 1, 2)),
            pltpu.SemaphoreType.DMA((2, REACH, 2)),
        ],
        compiler_params=pltpu.CompilerParams(collective_id=0, has_side_effects=True, vmem_limit_bytes=63 * 1024 * 1024),
    )(x, w_q, keys, values, cos_part, sin_part)


def solution(mesh):
    cp = mesh.shape["cp"]

    def device_step(hidden, w_q, w_k, w_v, w_o):
        me = lax.axis_index("cp")
        chunk_ids = jnp.stack([me, 2 * cp - 1 - me])
        positions = (chunk_ids[:, None] * CHUNK + jnp.arange(CHUNK)[None, :]).reshape(2 * CHUNK)
        cos_part, sin_part = rotation(positions)
        keys, values = project_kv(hidden, w_k, w_v, cos_part, sin_part)
        attended = attend(cp, hidden, w_q, keys, values, cos_part, sin_part)
        out = jnp.dot(attended, w_o.reshape(HEADS * DIM, hidden.shape[1]), preferred_element_type=jnp.float32)
        return out.astype(jnp.bfloat16)

    return jax.shard_map(device_step, mesh=mesh, in_specs=(P(("dp", "cp"), None), P(), P(), P(), P()), out_specs=P(("dp", "cp"), None), check_vma=False)
```

time: 219 us -> 143 us (0.65)
  the two profiles are of different devices: /device:TPU:1 before, /device:TPU:64 now
where the time goes in v2:
time: 143 us
  Pallas kernels  123 us (86%)
  matrix products  15.8 us (11%)
  local copies, waits for them, and re-layouts  3.01 us (2%)
    pallas_call x1, Pallas kernels, attend(): pl.pallas_call(functools.partial(attention_kernel, cp), name='band_attent...  119 us
    dot_general x1, matrix products, device_step(): jnp.dot(attended, w_o.reshape(HEADS * DIM, hidden.shape[1]), preferred_el...  15.8 us
    pallas_call x1, Pallas kernels, project_kv(): pl.pallas_call(project_kernel, name='project_kv', out_shape=(jax.ShapeDty...  3.81 us
    unnamed x13, local copies, waits for them, and re-layouts  3.01 us

profile of v2, /device:TPU:64, one launch (start us, length us, event | category | flops | bytes accessed | tf_op | source)
XLA Modules:
  0.0 143.0 jit_solution(13697642973193337018)
XLA Ops:
  0.0 0.0 copy-start.2
  0.0 0.1 add_multiply_fusion
  0.1 0.1 convert_bitcast_fusion
  0.2 1.0 fusion
  1.2 0.2 pad_maximum_fusion
  1.4 0.0 copy-start
  1.4 0.0 copy-start.1
  1.4 0.0 copy-done.2
  1.4 0.0 copy-start.3
  1.4 1.6 %copy-done.3 = bf16[3072,2,128]{2,1,0:T(2,128)(2,1)S(1)} copy-done((bf16[3072,2,128]{2,1,0:T(2,128)(2,1)S(1)}, bf16[3072,2,128]{2,1,0:T(2,128)(2,1)}, u32[]{:S(2)}) %copy-start.3) | copy-done | bytes 1572888
  3.0 3.8 %project_kv.1 = (bf16[2,2,256,128]{3,2,1,0:T(8,128)(2,1)S(1)}, bf16[2,2,2,128,128]{4,3,2,1,0:T(8,128)(2,1)S(1)}) custom-call(bf16[512,3072]{1,0:T(8,128)(2,1)} %x_ref.3, bf16[3072,2,128]{2,1,0:T(2,128)(2,1)S(1)} %copy-done.2, bf16[3072,2,128]{2,1,0:T(2,128)(2,1)S(1)} %copy-done.3, f32[512,128]{1,0:T(8,128)S(1)} %get-tuple-element.12.cos_ref, ...), custom_call_target="tpu_custom_call" | custom-call | tf_op jit(solution)/shard_map/project_kv/pallas_call | solution.py:405
  6.8 0.0 copy-done
  6.8 0.0 copy-done.1
  6.8 0.0 copy-start.4
  6.8 0.7 copy-done.4
  7.5 0.0 copy-start.5
  7.5 0.7 copy-done.5
  8.2 118.9 %band_attention.1 = bf16[512,3072]{1,0:T(8,128)(2,1)} custom-call(bf16[512,3072]{1,0:T(8,128)(2,1)} %x_ref.3, bf16[3072,24,128]{2,1,0:T(8,128)(2,1)} %w_ref.1, bf16[2,2,256,128]{3,2,1,0:T(8,128)(2,1)} %copy-done.4, bf16[2,2,2,128,128]{4,3,2,1,0:T(8,128)(2,1)} %copy-done.5, f32[512,128]{1,0:T(8,128)} %copy-done, f32[512,128]{1,0:T(8,128)} %copy-done.1), custom_call_target="tpu_custom_call" | custom-call | tf_op jit(solution)/shard_map/band_attention/pallas_call | solution.py:420
  127.2 15.8 %convolution_convert_fusion = bf16[512,3072]{1,0:T(8,128)(2,1)} fusion(bf16[512,3072]{1,0:T(8,128)(2,1)} %band_attention.1, bf16[3072,3072]{1,0:T(8,128)(2,1)} %bitcast.9), kind=kOutput, calls=%fused_computation | convolution fusion | flops 9665249280 | bytes 25165824 | tf_op jit(solution)/shard_map/dot_general | solution.py:463
  (2 shorter events, 0.0 us)
Async XLA Ops:
  0.0 1.4 copy-start.2
  1.4 5.4 %copy-start = (f32[512,128]{1,0:T(8,128)}, f32[512,128]{1,0:T(8,128)S(1)}, u32[]{:S(2)}) copy-start(f32[512,128]{1,0:T(8,128)S(1)} %get-tuple-element.12.cos_ref) | copy-start | bytes 786436
  1.4 5.4 %copy-start.1 = (f32[512,128]{1,0:T(8,128)}, f32[512,128]{1,0:T(8,128)S(1)}, u32[]{:S(2)}) copy-start(f32[512,128]{1,0:T(8,128)S(1)} %get-tuple-element.13.sin_ref) | copy-start | bytes 786436
  1.4 1.6 %copy-start.3 = (bf16[3072,2,128]{2,1,0:T(2,128)(2,1)S(1)}, bf16[3072,2,128]{2,1,0:T(2,128)(2,1)}, u32[]{:S(2)}) copy-start(bf16[3072,2,128]{2,1,0:T(2,128)(2,1)} %wv_ref.1) | copy-start | bytes 4718596
  6.8 0.7 copy-start.4
  7.5 0.7 copy-start.5

commit v3 on v2

--- a/solution.py
+++ b/solution.py
@@ -13,7 +13,6 @@
 REACH = WINDOW // CHUNK
 GROUP = 4
 STEPS = REACH // GROUP
-PAIRS = 1
 HEADS = 24
 KV_HEADS = 2
 SHARE = HEADS // KV_HEADS
@@ -29,6 +28,7 @@
 SENDS = 8
 HEAD_TILE = 8
 K_BLOCK = 768
+PARTS = 2
 
 
 def rotation(positions):
@@ -42,7 +42,7 @@
     return op(values.reshape(values.shape[0] // 8, 8, values.shape[1]), axis=0)
 
 
-def attention_kernel(cp, x_ref, w_ref, k_ref, v_ref, cos_ref, sin_ref, o_ref, q_ref, w_in, w_a, w_b, kbuf, vbuf, s_a, s_b, p_a, p_b, x_a, x_b, al_a, al_b, acc, mrun, lrun, w_sem, send_sem, fwd_sem, recv_sem):
+def attention_kernel(cp, x_ref, w_ref, k_ref, v_ref, cos_ref, sin_ref, o_ref, q_ref, w_in, w_a, w_b, kbuf, vbuf, s_a, s_b, p_a, p_b, f_a, f_b, x_a, x_b, al_a, al_b, acc, mrun, lrun, w_sem, send_sem, fwd_sem, recv_sem):
     me = lax.axis_index("cp")
     even_of = (lax.rem(me, 2) == 0, lax.rem(me, 2) == 1)
     partner = me + 1 - 2 * lax.rem(me, 2)
@@ -158,11 +158,6 @@
                 arrive(role, offset)
                 launch(role, offset)
 
-    def receive_forwarded(role, group):
-        for slot in range(GROUP * group, GROUP * group + GROUP):
-            if OFFSETS[slot] % 2:
-                arrive(role, OFFSETS[slot])
-
     for slot, offset in enumerate(OFFSETS):
         @pl.when(me < offset)
         def _(slot=slot):
@@ -185,71 +180,82 @@
     for role in range(2):
         launch(role, "start")
 
-    def relayout(tile, block, w_out):
-        fetch(tile, block, block).wait()
-        rows = pl.ds(pl.multiple_of(block * K_BLOCK, K_BLOCK), K_BLOCK)
-        w_out[rows, :] = w_in[block].reshape(K_BLOCK, HEAD_TILE * DIM)
-
-    def project(tile, pair, w_two):
+    def relayout(block, part, w_out):
+        n = K_BLOCK // PARTS
+        rows = pl.ds(pl.multiple_of(block * K_BLOCK + part * n, n), n)
+        w_out[rows, :] = w_in[block, part * n : part * n + n].reshape(n, HEAD_TILE * DIM)
+
+    def project(tile, pair, part, w_two):
         cols = pl.ds(pl.multiple_of(pair * 2 * DIM, 2 * DIM), 2 * DIM)
-        found = jnp.dot(x_ref[...], w_two[:, cols], preferred_element_type=jnp.float32).astype(jnp.bfloat16).astype(jnp.float32)
+        n = 2 * CHUNK // PARTS
+        rows = slice(part * n, part * n + n)
+        found = jnp.dot(x_ref[rows, :], w_two[:, cols], preferred_element_type=jnp.float32).astype(jnp.bfloat16).astype(jnp.float32)
         for k in range(2):
             q = found[:, k * DIM : k * DIM + DIM]
-            q = (q * cos_ref[...] + pltpu.roll(q, DIM // 2, 1) * sin_ref[...]) * jnp.float32(DIM ** -0.5)
-            q = q.astype(jnp.bfloat16)
-            h = tile * HEAD_TILE + 2 * pair + k
-            q_ref[h] = q[:CHUNK]
-            q_ref[HEADS + h] = q[CHUNK:]
+            q = (q * cos_ref[rows, :] + pltpu.roll(q, DIM // 2, 1) * sin_ref[rows, :]) * jnp.float32(DIM ** -0.5)
+            chunk, start = divmod(part * n, CHUNK)
+            q_ref[chunk * HEADS + tile * HEAD_TILE + 2 * pair + k, start : start + n] = q.astype(jnp.bfloat16)
 
     w_two = (w_a, w_b)
     for tile in range(n_tiles + 1):
         def body(block, carry, tile=tile):
             if tile < n_tiles:
-                relayout(tile, block, w_two[tile % 2])
-                if tile + 1 < n_tiles:
-                    fetch(tile + 1, block, block).start()
-            if tile:
-                project(tile - 1, block, w_two[(tile - 1) % 2])
+                fetch(tile, block, block).wait()
+            for part in range(PARTS):
+                if tile:
+                    project(tile - 1, block, part, w_two[(tile - 1) % 2])
+                if tile < n_tiles:
+                    relayout(block, part, w_two[tile % 2])
+            if tile + 1 < n_tiles:
+                fetch(tile + 1, block, block).start()
             return carry
         lax.fori_loop(0, n_blocks, body, 0)
         if tile == 1:
             relay(8)
     relay(16, 2, 6)
 
-    key_ids = lax.broadcasted_iota(jnp.int32, (CHUNK, CHUNK), 0)
-    query_ids = lax.broadcasted_iota(jnp.int32, (CHUNK, CHUNK), 1)
-
-    def query(role, h):
-        return q_ref[role * HEADS + h]
+    causal = lax.broadcasted_iota(jnp.int32, (HALF, HALF), 0) <= lax.broadcasted_iota(jnp.int32, (HALF, HALF), 1)
+    LOW, HIGH = slice(0, HALF), slice(HALF, CHUNK)
 
     def scores(keys, qh):
         return lax.dot_general(keys, qh, (((1,), (1,)), ((), ())), preferred_element_type=jnp.float32)
 
-    def bias_of(role, slot, offset):
+    def bias_of(role, group, c):
+        if isinstance(role, int) and role:
+            return None
+        offset = OFFSETS[GROUP * group + c] if isinstance(group, int) else jnp.where(
+            group == 1, OFFSETS[GROUP + c], jnp.where(group == 2, OFFSETS[2 * GROUP + c], OFFSETS[3 * GROUP + c]))
         return jnp.where(jnp.logical_and(role == 0, me < offset), jnp.float32(NEG), jnp.float32(0))
 
-    def offset_of(group, c):
-        return jnp.where(group == 1, OFFSETS[GROUP + c], jnp.where(group == 2, OFFSETS[2 * GROUP + c], OFFSETS[3 * GROUP + c]))
+    def plus(value, bias):
+        return value if bias is None else value + bias
 
     def stage_qk(role, group, h, s_ref, x_ref, first):
         kv = h // SHARE
-        qh = query(role, h)
+        qh = q_ref[role * HEADS + h]
         top = None
         for c in range(GROUP):
-            slot = GROUP * group + c
-            s = scores(kbuf[role, kv, slot], qh)
+            s = scores(kbuf[role, kv, GROUP * group + c], qh)
+            bias = bias_of(role, group, c)
             if first and c == 0:
                 own = scores(k_ref[role, kv], qh)
-                s = jnp.where(key_ids <= query_ids, own, s + bias_of(role, slot, REACH))
-                part = fold8(s, jnp.max)
+                low = jnp.where(causal, own[LOW, LOW], plus(s[LOW, LOW], bias))
+                high = jnp.where(causal, own[HIGH, HIGH], plus(s[HIGH, HIGH], bias))
+                s_ref[LOW, LOW] = low
+                s_ref[HIGH, HIGH] = high
+                s_ref[LOW, HIGH] = own[LOW, HIGH]
+                s_ref[HIGH, LOW] = s[HIGH, LOW]
+                left = jnp.maximum(fold8(low, jnp.max), plus(fold8(s[HIGH, LOW], jnp.max), bias))
+                right = jnp.maximum(fold8(own[LOW, HIGH], jnp.max), fold8(high, jnp.max))
+                part = jnp.concatenate([left, right], axis=1)
             else:
-                offset = OFFSETS[c] if first else offset_of(group, c)
-                part = fold8(s, jnp.max) + bias_of(role, slot, offset)
-            s_ref[pl.ds(c * CHUNK, CHUNK), :] = s
+                part = plus(fold8(s, jnp.max), bias)
+                s_ref[pl.ds(c * CHUNK, CHUNK), :] = s
             top = part if top is None else jnp.maximum(top, part)
+            yield
         x_ref[...] = top
 
-    def stage_softmax(role, group, h, s_ref, x_ref, p_ref, al_ref, first):
+    def stage_softmax(role, group, h, s_ref, x_ref, p_ref, al_ref, f_ref, first):
         row = role * HEADS + h
         top = jnp.max(x_ref[...], axis=0, keepdims=True)
         if first:
@@ -262,21 +268,33 @@
         mrun[row] = jnp.broadcast_to(m, (8, CHUNK))
         sums = [None, None]
         for c in range(GROUP):
-            slot = GROUP * group + c
-            shift = m
-            if not (first and c == 0):
-                shift = m - bias_of(role, slot, OFFSETS[c] if first else offset_of(group, c))
-            for half in range(2):
-                cols = slice(half * HALF, half * HALF + HALF)
-                for r in range(c * CHUNK, c * CHUNK + CHUNK, PIECE):
-                    e = jnp.exp(s_ref[r : r + PIECE, cols] - shift[:, cols])
+            bias = bias_of(role, group, c)
+            shifted = m if bias is None else m - bias
+            for r in range(0, CHUNK, PIECE):
+                for half in range(2):
+                    cols = slice(half * HALF, half * HALF + HALF)
+                    rows = slice(c * CHUNK + r, c * CHUNK + r + PIECE)
+                    lower = r >= HALF
+                    edge = first and c == 0
+                    shift = m if edge and not (lower and half == 0) else shifted
+                    e = jnp.exp(s_ref[rows, cols] - shift[:, cols])
                     part = fold8(e, jnp.sum)
                     sums[half] = part if sums[half] is None else sums[half] + part
-                    p_ref[half, r : r + PIECE] = e.astype(jnp.bfloat16)
+                    if not edge:
+                        p_ref[half, rows] = e.astype(jnp.bfloat16)
+                    elif lower and half == 0:
+                        f_ref[half, rows] = e.astype(jnp.bfloat16)
+                    elif not lower and half == 1:
+                        p_ref[half, rows] = e.astype(jnp.bfloat16)
+                    else:
+                        mask = causal[r % HALF : r % HALF + PIECE]
+                        p_ref[half, rows] = jnp.where(mask, e, 0.0).astype(jnp.bfloat16)
+                        f_ref[half, rows] = jnp.where(mask, 0.0, e).astype(jnp.bfloat16)
+            yield
         total = jnp.concatenate(sums, axis=1)
         lrun[row] = total if first else lrun[row] * alpha + total
 
-    def stage_pv(role, group, h, row, p_ref, al_ref, first):
+    def stage_pv(role, group, h, row, p_ref, al_ref, f_ref, first):
         kv = h // SHARE
         out = None
         for c in range(GROUP):
@@ -285,87 +303,90 @@
             p = jnp.concatenate([p_ref[0, rows], p_ref[1, rows]], axis=1)
             values = jnp.concatenate([vbuf[role, kv, slot, 0], vbuf[role, kv, slot, 1]], axis=1)
             if first and c == 0:
-                causal = key_ids <= query_ids
-                none = jnp.zeros_like(p)
                 own = jnp.concatenate([v_ref[role, kv, 0], v_ref[role, kv, 1]], axis=1)
-                part = jnp.dot(own, jnp.where(causal, p, none), preferred_element_type=jnp.float32)
-                part += jnp.dot(values, jnp.where(causal, none, p), preferred_element_type=jnp.float32)
+                far = jnp.concatenate([f_ref[0], f_ref[1]], axis=1)
+                out = jnp.dot(own, p, preferred_element_type=jnp.float32)
+                out += jnp.dot(values, far, preferred_element_type=jnp.float32)
             else:
                 part = jnp.dot(values, p, preferred_element_type=jnp.float32)
-            out = part if out is None else out + part
+                out = part if out is None else out + part
+            yield
         if first:
             acc[row] = out
         else:
             acc[row] = acc[row] * al_ref[0:1] + out
 
-    TRIPS = HEADS // (2 * PAIRS)
-
-    def run(first_step, n_steps, first, receive):
-        n_units = n_steps * HEADS
-
-        def place(unit):
-            step = first_step + unit // HEADS
-            return lax.rem(step, 2), step // 2, lax.rem(unit, HEADS)
-
-        def qk(unit, s_ref, x_ref):
-            stage_qk(*place(unit), s_ref, x_ref, first)
-
-        def softmax(unit, *refs):
-            stage_softmax(*place(unit), *refs, first)
-
-        def pv(unit, row, *refs):
-            role, group, h = place(unit)
-            stage_pv(role, group, h, row, *refs, first)
-
-        def row_of(unit):
-            role, _, h = place(unit)
-            return role * HEADS + h
-
-        qk(0, s_a, x_a)
-
-        def body(i, carry):
-            receive(i)
-            for pair in range(PAIRS):
-                unit = 2 * (PAIRS * i + pair)
-                before = jnp.maximum(unit - 1, 0) if pair == 0 else unit - 1
-                after = jnp.minimum(unit + 2, n_units - 1) if pair == PAIRS - 1 else unit + 2
-                row = jnp.where(i == 0, 2 * HEADS, row_of(before)) if pair == 0 else row_of(before)
-                qk(unit + 1, s_b, x_b)
-                softmax(unit, s_a, x_a, p_a, al_a)
-                pv(before, row, p_b, al_b)
-                qk(after, s_a, x_a)
-                softmax(unit + 1, s_b, x_b, p_b, al_b)
-                pv(unit, row_of(unit), p_a, al_a)
-            return carry
-
-        lax.fori_loop(0, n_units // (2 * PAIRS), body, 0)
-        pv(n_units - 1, row_of(n_units - 1), p_b, al_b)
+    TRIPS = HEADS // 2
+
+    def weave(*stages):
+        stages = list(stages)
+        while stages:
+            stages = [stage for stage in stages if next(stage, stages) is None]
+
+    def run(steps, first, ready):
+        ready(0)
+        weave(stage_qk(*steps[0], 0, s_a, x_a, first))
+        for index, (role, group) in enumerate(steps):
+            before = steps[index - 1] if index else (role, group)
+            after = steps[index + 1] if index + 1 < len(steps) else (role, group)
+
+            def body(i, carry, index=index, role=role, group=group, before=before, after=after):
+                if index + 1 < len(steps):
+                    @pl.when(i == TRIPS - 1)
+                    def _():
+                        receive_forwarded(*after)
+                h = 2 * i
+                head, last = i == 0, i == TRIPS - 1
+                pick = lambda cond, a, b: b if isinstance(a, int) and isinstance(b, int) and a == b else jnp.where(cond, a, b)
+                b_role, b_group = pick(head, before[0], role), pick(head, before[1], group)
+                b_h = jnp.where(head, HEADS - 1, h - 1)
+                b_row = b_role * HEADS + b_h
+                if index == 0:
+                    b_row = jnp.where(head, 2 * HEADS, b_row)
+                a_role, a_group = pick(last, after[0], role), pick(last, after[1], group)
+                a_h = jnp.where(last, 0, h + 2)
+                weave(
+                    stage_softmax(role, group, h, s_a, x_a, p_a, al_a, f_a, first),
+                    stage_qk(role, group, h + 1, s_b, x_b, first),
+                    stage_pv(b_role, b_group, b_h, b_row, p_b, al_b, f_b, first),
+                )
+                weave(
+                    stage_softmax(role, group, h + 1, s_b, x_b, p_b, al_b, f_b, first),
+                    stage_qk(a_role, a_group, a_h, s_a, x_a, first),
+                    stage_pv(role, group, h, role * HEADS + h, p_a, al_a, f_a, first),
+                )
+                return carry
+
+            if index:
+                ready(index)
+            lax.fori_loop(0, TRIPS, body, 0)
+        role, group = steps[-1]
+        weave(stage_pv(role, group, HEADS - 1, role * HEADS + HEADS - 1, p_b, al_b, f_b, first))
+
+    def receive_forwarded(role, group):
+        for offset in OFFSETS[GROUP * group : GROUP * group + GROUP]:
+            if offset % 2:
+                arrive(role, offset)
+
+    def ready_first(index):
+        if index:
+            relay(10)
+
+    def ready_rest(index):
+        if index == 0:
+            relay(14)
+            receive_forwarded(0, 1)
+        if index == 1:
+            relay(4)
+        if index == 2:
+            relay(12)
 
     receive_forwarded(0, 0)
-
-    def at(trip, i, fn):
-        @pl.when(i == trip)
-        def _():
-            fn()
-
-    def receive_first(i):
-        at(TRIPS // 2, i, lambda: relay(10))
-        at(TRIPS - 1, i, lambda: receive_forwarded(1, 0))
-        at(TRIPS + TRIPS // 4, i, lambda: relay(14))
-
-    def receive_rest(i):
-        at(0, i, lambda: relay(4))
-        at(TRIPS, i, lambda: relay(12))
-        for step in range(2 * STEPS - 3):
-            group, role = divmod(step + 3, 2)
-            at(TRIPS * step + TRIPS - 1, i, lambda role=role, group=group: receive_forwarded(role, group))
-
-    p_b[...] = jnp.zeros_like(p_b)
-    al_b[...] = jnp.zeros_like(al_b)
+    for ref in (p_a, p_b, f_a, f_b, al_b):
+        ref[...] = jnp.zeros_like(ref)
     acc[2 * HEADS] = jnp.zeros((DIM, CHUNK), jnp.float32)
-    run(0, 2, True, receive_first)
-    receive_forwarded(0, 1)
-    run(2, 2 * STEPS - 2, False, receive_rest)
+    run([(0, 0), (1, 0)], True, ready_first)
+    run([(role, group) for group in range(1, STEPS) for role in range(2)], False, ready_rest)
 
     def finish(j, carry):
         for k in range(2):
@@ -434,6 +455,8 @@
             pltpu.VMEM((GROUP * CHUNK, CHUNK), f32),
             pltpu.VMEM((2, GROUP * CHUNK, HALF), bf16),
             pltpu.VMEM((2, GROUP * CHUNK, HALF), bf16),
+            pltpu.VMEM((2, CHUNK, HALF), bf16),
+            pltpu.VMEM((2, CHUNK, HALF), bf16),
             pltpu.VMEM((8, CHUNK), f32),
             pltpu.VMEM((8, CHUNK), f32),
             pltpu.VMEM((8, CHUNK), f32),
@@ -450,6 +473,23 @@
     )(x, w_q, keys, values, cos_part, sin_part)
 
 
+def out_kernel(x_ref, w_ref, y_ref):
+    y_ref[...] = jnp.dot(x_ref[...], w_ref[...], preferred_element_type=jnp.float32).astype(jnp.bfloat16)
+
+
+def project_out(attended, w, columns=256):
+    rows, depth = attended.shape
+    return pl.pallas_call(
+        out_kernel,
+        name="project_out",
+        grid=(w.shape[1] // columns,),
+        out_shape=jax.ShapeDtypeStruct((rows, w.shape[1]), jnp.bfloat16),
+        in_specs=[pl.BlockSpec((rows, depth), lambda n: (0, 0)), pl.BlockSpec((depth, columns), lambda n: (0, n))],
+        out_specs=pl.BlockSpec((rows, columns), lambda n: (0, n)),
+        compiler_params=pltpu.CompilerParams(vmem_limit_bytes=48 * 1024 * 1024),
+    )(attended, w)
+
+
 def solution(mesh):
     cp = mesh.shape["cp"]
 
@@ -460,7 +500,6 @@
         cos_part, sin_part = rotation(positions)
         keys, values = project_kv(hidden, w_k, w_v, cos_part, sin_part)
         attended = attend(cp, hidden, w_q, keys, values, cos_part, sin_part)
-        out = jnp.dot(attended, w_o.reshape(HEADS * DIM, hidden.shape[1]), preferred_element_type=jnp.float32)
-        return out.astype(jnp.bfloat16)
+        return project_out(attended, w_o.reshape(HEADS * DIM, hidden.shape[1]))
 
     return jax.shard_map(device_step, mesh=mesh, in_specs=(P(("dp", "cp"), None), P(), P(), P(), P()), out_specs=P(("dp", "cp"), None), check_vma=False)

time: 143 us -> 153 us (1.070)
  the two profiles are of different devices: /device:TPU:64 before, /device:TPU:98 now
where the time goes in v3:
time: 153 us; the launch traced here: 152 us
  Pallas kernels  146 us (95%)
  local copies, waits for them, and re-layouts  4.89 us (3%)
    pallas_call x1, Pallas kernels, attend(): pl.pallas_call(functools.partial(attention_kernel, cp), name='band_attent...  125 us
    pallas_call x1, Pallas kernels, project_out(): pl.pallas_call(out_kernel, name='project_out', grid=(w.shape[1] // column...  17 us
    unnamed x15, local copies, waits for them, and re-layouts  4.89 us
    pallas_call x1, Pallas kernels, project_kv(): pl.pallas_call(project_kernel, name='project_kv', out_shape=(jax.ShapeDty...  3.81 us

profile of v3, /device:TPU:98, one launch (start us, length us, event | category | flops | bytes accessed | tf_op | source)
XLA Modules:
  0.0 152.2 jit_solution(1710218398451503002)
XLA Ops:
  0.0 0.0 copy-start.3
  0.0 0.1 add_multiply_fusion
  0.1 0.1 convert_bitcast_fusion
  0.2 1.0 fusion
  1.2 0.2 pad_maximum_fusion
  1.4 0.0 copy-start.1
  1.4 0.0 copy-start.2
  1.4 0.0 copy-done.3
  1.4 0.0 copy-start.4
  1.4 1.6 %copy-done.4 = bf16[3072,2,128]{2,1,0:T(2,128)(2,1)S(1)} copy-done((bf16[3072,2,128]{2,1,0:T(2,128)(2,1)S(1)}, bf16[3072,2,128]{2,1,0:T(2,128)(2,1)}, u32[]{:S(2)}) %copy-start.4) | copy-done | bytes 1572888
  3.0 3.8 %project_kv.1 = (bf16[2,2,256,128]{3,2,1,0:T(8,128)(2,1)S(1)}, bf16[2,2,2,128,128]{4,3,2,1,0:T(8,128)(2,1)S(1)}) custom-call(bf16[512,3072]{1,0:T(8,128)(2,1)} %x_ref.3, bf16[3072,2,128]{2,1,0:T(2,128)(2,1)S(1)} %copy-done.3, bf16[3072,2,128]{2,1,0:T(2,128)(2,1)S(1)} %copy-done.4, f32[512,128]{1,0:T(8,128)S(1)} %get-tuple-element.12.cos_ref, ...), custom_call_target="tpu_custom_call" | custom-call | tf_op jit(solution)/shard_map/project_kv/pallas_call | solution.py:426
  6.8 0.0 copy-done.1
  6.8 0.0 copy-done.2
  6.8 0.0 copy-start.5
  6.8 0.7 copy-done.5
  7.5 0.0 copy-start.6
  7.5 0.7 copy-done.6
  8.2 125.1 %band_attention.1.x_ref = bf16[512,3072]{1,0:T(8,128)(2,1)} custom-call(bf16[512,3072]{1,0:T(8,128)(2,1)} %x_ref.3, bf16[3072,24,128]{2,1,0:T(8,128)(2,1)} %w_ref.1, bf16[2,2,256,128]{3,2,1,0:T(8,128)(2,1)} %copy-done.5, bf16[2,2,2,128,128]{4,3,2,1,0:T(8,128)(2,1)} %copy-done.6, f32[512,128]{1,0:T(8,128)} %copy-done.1, f32[512,128]{1,0:T(8,128)} %copy-done.2), custom_call_target="tpu_custom_call" | custom-call | tf_op jit(solution)/shard_map/band_attention/pallas_call | solution.py:441
  133.3 0.0 copy-start
  133.3 1.9 %copy-done = bf16[512,3072]{1,0:T(8,128)(2,1)S(1)} copy-done((bf16[512,3072]{1,0:T(8,128)(2,1)S(1)}, bf16[512,3072]{1,0:T(8,128)(2,1)}, u32[]{:S(2)}) %copy-start) | copy-done | bytes 3145752
  135.2 17.0 %project_out.1 = bf16[512,3072]{1,0:T(8,128)(2,1)} custom-call(bf16[512,3072]{1,0:T(8,128)(2,1)S(1)} %copy-done, bf16[3072,3072]{1,0:T(8,128)(2,1)} %bitcast.6), custom_call_target="tpu_custom_call" | custom-call | tf_op jit(solution)/shard_map/project_out/pallas_call | solution.py:482
  (2 shorter events, 0.0 us)
Async XLA Ops:
  0.0 1.4 copy-start.3
  1.4 5.4 %copy-start.1 = (f32[512,128]{1,0:T(8,128)}, f32[512,128]{1,0:T(8,128)S(1)}, u32[]{:S(2)}) copy-start(f32[512,128]{1,0:T(8,128)S(1)} %get-tuple-element.12.cos_ref) | copy-start | bytes 786436
  1.4 5.4 %copy-start.2 = (f32[512,128]{1,0:T(8,128)}, f32[512,128]{1,0:T(8,128)S(1)}, u32[]{:S(2)}) copy-start(f32[512,128]{1,0:T(8,128)S(1)} %get-tuple-element.13.sin_ref) | copy-start | bytes 786436
  1.4 1.6 %copy-start.4 = (bf16[3072,2,128]{2,1,0:T(2,128)(2,1)S(1)}, bf16[3072,2,128]{2,1,0:T(2,128)(2,1)}, u32[]{:S(2)}) copy-start(bf16[3072,2,128]{2,1,0:T(2,128)(2,1)} %wv_ref.1) | copy-start | bytes 4718596
  6.8 0.7 copy-start.5
  7.5 0.7 copy-start.6
  133.3 1.9 %copy-start = (bf16[512,3072]{1,0:T(8,128)(2,1)S(1)}, bf16[512,3072]{1,0:T(8,128)(2,1)}, u32[]{:S(2)}) copy-start(bf16[512,3072]{1,0:T(8,128)(2,1)} %band_attention.1.x_ref) | copy-start | bytes 9437188
